TPU v7x, 128 devices: a whole 4x4x4 slice. The times are simulated.
128 devices in a mesh: dp: 1, cp: 128 (over z, y, x, core).
Axes of the slice: x: 4, y: 4, z: 4, core: 2. Of those that a mesh axis runs over, the one named last changes fastest.
Arguments:
- x_seq: bfloat16 [1, 32768, 1024], P('dp', 'cp')
- w_in: bfloat16 [1024, 3072], replicated
- w_out: bfloat16 [1024, 1024], replicated
- filt_taps: float32 [32768, 1024], replicated
- skip_gain: float32 [1024], replicated
- d_out: bfloat16 [1, 32768, 1024], P('dp', 'cp')
Outputs:
- output 1: bfloat16 [1, 32768, 1024], P('dp', 'cp')
- output 2: bfloat16 [1024, 3072], P(('dp', 'cp'))
- output 3: bfloat16 [1024, 1024], P(('dp', 'cp'))
- output 4: float32 [32768, 1024], P('dp', 'cp')
- output 5: float32 [1024], P(('dp', 'cp'))
All inputs are finite; a program needn't handle non-finite values.
Results may differ from a plain program's by a relative error of at most 0.0113872.
Values are sent between devices in bfloat16 or wider.
A program may use at most 1 GiB of HBM per device.

v0:
```python
import functools

import jax
import jax.numpy as jnp
import numpy as np
from jax import lax
from jax.experimental import pallas as pl
from jax.experimental.pallas import tpu as pltpu
from jax.sharding import PartitionSpec as P

F32, BF16 = jnp.float32, jnp.bfloat16


def split_const(mat):
    hi = mat.astype(np.float32).astype(jnp.bfloat16)
    lo = (mat - hi.astype(np.float64)).astype(np.float32).astype(jnp.bfloat16)
    return hi, lo


@functools.lru_cache(None)
def transform_tables(n_rows, n_lanes):
    n = n_rows * n_lanes
    t1 = np.concatenate([np.arange(0, n_rows, 2), np.arange(1, n_rows, 2)])
    k1 = np.arange(n_rows)
    ang = 2 * np.pi * np.outer(k1 + 0.25, t1) / n_rows
    f1 = np.concatenate([np.cos(ang), -np.sin(ang)], axis=0)
    g1 = f1.T / n
    t2 = np.arange(n_lanes)
    psi = 2 * np.pi * (np.outer(t2, t2) % n_lanes) / n_lanes
    cos2, sin2 = np.cos(psi), np.sin(psi)
    f2 = np.block([[cos2, -sin2], [sin2, cos2]])
    g2 = f2.T
    twist = 2 * np.pi * np.outer(k1 + 0.25, t2) / n
    twid = np.concatenate([np.cos(twist), -np.sin(twist)], axis=1).astype(np.float32)
    f1h, f1l = split_const(f1)
    g1h, g1l = split_const(g1)
    f2h, f2l = split_const(f2)
    g2h, g2l = split_const(g2)
    return (
        np.concatenate([f1h, f1l], axis=1),
        np.concatenate([f2h, f2l], axis=0),
        np.concatenate([g2h, g2l], axis=0),
        np.concatenate([g1h, g1l], axis=1),
        twid,
    )


def dot(a, b):
    return jnp.dot(a, b, preferred_element_type=F32)


def halves(val):
    hi = val.astype(BF16)
    lo = (val - hi.astype(F32)).astype(BF16)
    return hi, lo


def conv_kernel(n_chans, sig_ref, filt_ref, skip_ref, f1_ref, f2_ref, g2_ref, g1_ref, tw_ref,
                out_ref, gfilt_ref, gskip_ref, sig_f32, out_f32):
    n_src = sig_ref.shape[0]
    n_rows, n_lanes = 2 * n_src, sig_ref.shape[2] // 2
    for half in range(2):
        sig_f32[half] = sig_ref[:, :, half * n_lanes:(half + 1) * n_lanes].astype(F32).reshape(sig_f32.shape[1:])

    def rows_of(chan):
        val = jnp.concatenate([sig_f32[0, pl.ds(chan, n_src, stride=2 * n_chans), :],
                               sig_f32[1, pl.ds(chan, n_src, stride=2 * n_chans), :]], axis=0)
        return val

    def taps_of(chan):
        return jnp.concatenate([filt_ref[pl.ds(chan, n_src, stride=2 * n_chans), :],
                                filt_ref[pl.ds(n_chans + chan, n_src, stride=2 * n_chans), :]], axis=0)

    wr, wi = tw_ref[:, :n_lanes], tw_ref[:, n_lanes:]
    f1h, f1l = f1_ref[:, :n_rows], f1_ref[:, n_rows:]
    f2h, f2l = f2_ref[:2 * n_lanes], f2_ref[2 * n_lanes:]
    g2h, g2l = g2_ref[:2 * n_lanes], g2_ref[2 * n_lanes:]
    g1h, g1l = g1_ref[:, :2 * n_rows], g1_ref[:, 2 * n_rows:]

    def second(stage):
        parts = []
        for i in range(2):
            ar = stage[:n_rows, i * n_lanes:(i + 1) * n_lanes]
            ai = stage[n_rows:, i * n_lanes:(i + 1) * n_lanes]
            parts.append(jnp.concatenate([ar * wr - ai * wi, ar * wi + ai * wr], axis=1))
        bh, bl = halves(jnp.concatenate(parts, axis=0))
        spec = dot(bh, f2h) + (dot(bh, f2l) + dot(bl, f2h))
        return spec[:, :n_lanes], spec[:, n_lanes:]

    def inverse(pr, pi):
        ph, pll = halves(jnp.concatenate([pr, pi], axis=1))
        mid = dot(ph, g2h) + (dot(ph, g2l) + dot(pll, g2h))
        tr, ti = [], []
        for i in range(2):
            gr = mid[i * n_rows:(i + 1) * n_rows, :n_lanes]
            gi = mid[i * n_rows:(i + 1) * n_rows, n_lanes:]
            tr.append(gr * wr + gi * wi)
            ti.append(gi * wr - gr * wi)
        th, tl = halves(jnp.concatenate([jnp.concatenate(tr, axis=1), jnp.concatenate(ti, axis=1)], axis=0))
        return dot(g1h, th) + (dot(g1h, tl) + dot(g1l, th))

    def pair(step, carry):
        c0 = 2 * step
        u_val = jnp.concatenate([rows_of(c0), rows_of(c0 + 1)], axis=1)
        dy_val = jnp.concatenate([rows_of(n_chans + c0), rows_of(n_chans + c0 + 1)], axis=1)
        h_val = jnp.concatenate([taps_of(c0), taps_of(c0 + 1)], axis=1)
        u_bf, dy_bf = u_val.astype(BF16), dy_val.astype(BF16)
        h_hi, h_lo = halves(h_val)
        ur, ui = second(dot(f1h, u_bf) + dot(f1l, u_bf))
        dr, di = second(dot(f1h, dy_bf) + dot(f1l, dy_bf))
        hr, hi = second(dot(f1h, h_hi) + (dot(f1h, h_lo) + dot(f1l, h_hi)))
        y_lin = inverse(ur * hr - ui * hi, ur * hi + ui * hr)
        du_lin = inverse(dr * hr + di * hi, di * hr - dr * hi)
        gh_lin = inverse(dr * ur + di * ui, di * ur - dr * ui)
        for i in range(2):
            chan = c0 + i
            cols = slice(i * n_lanes, (i + 1) * n_lanes)
            skip = skip_ref[chan]
            y_out = (y_lin[:, cols] + skip * u_val[:, cols]).astype(BF16).astype(F32)
            du_out = (du_lin[:, cols] + skip * dy_val[:, cols]).astype(BF16).astype(F32)
            gskip_ref[pl.ds(chan, 1), :] = jnp.sum(u_val[:, cols] * dy_val[:, cols], axis=0, keepdims=True)
            for odd in range(2):
                rows = slice(odd * n_src, (odd + 1) * n_src)
                out_f32[odd, pl.ds(chan, n_src, stride=2 * n_chans), :] = y_out[rows]
                out_f32[odd, pl.ds(n_chans + chan, n_src, stride=2 * n_chans), :] = du_out[rows]
                gfilt_ref[pl.ds(odd * n_chans + chan, n_src, stride=2 * n_chans), :] = gh_lin[rows, cols]
        return carry

    lax.fori_loop(0, n_chans // 2, pair, 0)
    for half in range(2):
        out_ref[:, :, half * n_lanes:(half + 1) * n_lanes] = out_f32[half].astype(BF16).reshape(
            n_src, 2 * n_chans, n_lanes)


def channel_convs(sig, taps, skip):
    n_src, n_both, n_tok = sig.shape
    n_chans, n_lanes = n_both // 2, n_tok // 2
    n_rows = 2 * n_src
    tables = transform_tables(n_rows, n_lanes)
    vmem = pl.BlockSpec(memory_space=pltpu.VMEM)
    return pl.pallas_call(
        functools.partial(conv_kernel, n_chans),
        out_shape=(
            jax.ShapeDtypeStruct(sig.shape, BF16),
            jax.ShapeDtypeStruct((n_rows * n_chans, n_lanes), F32),
            jax.ShapeDtypeStruct((n_chans, n_lanes), F32),
        ),
        in_specs=[vmem, vmem, pl.BlockSpec(memory_space=pltpu.SMEM)] + [vmem] * 5,
        out_specs=(vmem, vmem, vmem),
        scratch_shapes=[
            pltpu.VMEM((2, n_src * n_both, n_lanes), F32),
            pltpu.VMEM((2, n_src * n_both, n_lanes), F32),
        ],
        compiler_params=pltpu.CompilerParams(vmem_limit_bytes=48 * 2 ** 20),
        cost_estimate=pl.CostEstimate(flops=10 ** 10, bytes_accessed=8 * 2 ** 20, transcendentals=0),
        name="channel_convs",
    )(sig, taps, skip, *[jnp.asarray(tab) for tab in tables])


def solution(mesh):
    ctx_size = mesh.shape["cp"]

    def local_step(x_seq, w_in, w_out, filt_taps, skip_gain, d_out):
        n_batch, n_tok, width = x_seq.shape
        n_chans = width // ctx_size
        seq_len = n_tok * ctx_size
        n_lanes = n_tok // 2
        rank = lax.axis_index("cp")
        x_tok, do_tok = x_seq[0], d_out[0]

        def mm(a, b, ca, cb):
            return lax.dot_general(a, b, (((ca,), (cb,)), ((), ())), preferred_element_type=F32)

        qkv = mm(w_in, x_tok, 0, 1).astype(BF16)
        q_act, k_act, v_act = qkv[:width], qkv[width:2 * width], qkv[2 * width:]
        u_act = k_act * v_act
        dz_act = mm(w_out, do_tok, 1, 1).astype(BF16)
        dy_act = dz_act * q_act
        sig = jnp.concatenate([u_act.reshape(ctx_size, n_chans, n_tok), dy_act.reshape(ctx_size, n_chans, n_tok)], axis=1)
        sig = lax.all_to_all(sig, "cp", 0, 0, tiled=True)

        taps = lax.dynamic_slice_in_dim(filt_taps, rank * n_chans, n_chans, axis=1)
        taps = taps.reshape(seq_len // n_lanes, n_lanes, n_chans).transpose(0, 2, 1).reshape(-1, n_lanes)
        skip = lax.dynamic_slice_in_dim(skip_gain, rank * n_chans, n_chans, axis=0)
        res, gfilt, gskip = channel_convs(sig, taps, skip)
        grad_filt = gfilt.reshape(seq_len // n_lanes, n_chans, n_lanes).transpose(0, 2, 1).reshape(seq_len, n_chans)
        grad_skip = jnp.sum(gskip, axis=1)

        res = lax.all_to_all(res, "cp", 0, 0, tiled=True)
        y_act = res[:, :n_chans].reshape(width, n_tok)
        du_act = res[:, n_chans:].reshape(width, n_tok)
        z_act = q_act * y_act
        d_qkv = jnp.concatenate([dz_act * y_act, du_act * v_act, du_act * k_act], axis=0)
        grad_x = mm(d_qkv, w_in, 0, 1).astype(BF16)[None]
        dw_in = mm(x_tok, d_qkv, 0, 1)
        dw_out = mm(z_act, do_tok, 1, 0)
        parts = jnp.concatenate([dw_in, dw_out], axis=1).reshape(ctx_size, n_chans, 4 * width)
        parts = lax.all_to_all(parts, "cp", 0, 0, tiled=True)
        sums = jnp.sum(parts, axis=0).astype(BF16)
        return grad_x, sums[:, :3 * width], sums[:, 3 * width:], grad_filt, grad_skip

    seq_spec = P("dp", "cp", None)
    row_spec = P(("dp", "cp"), None)
    return jax.shard_map(
        local_step,
        mesh=mesh,
        in_specs=(seq_spec, P(), P(), P(), P(), seq_spec),
        out_specs=(seq_spec, row_spec, row_spec, P("dp", "cp"), P(("dp", "cp"))),
        check_vma=False,
    )
```

profile of v0, /device:TPU:11, one launch (start us, length us, event | category | flops | bytes accessed | tf_op | source)
XLA Modules:
  0.0 386.4 jit_solution(12778948402136256995)
XLA Ops:
  0.6 0.0 copy-start
  0.6 0.0 copy-start.11
  0.7 1.6 copy-done
  2.2 1.8 convolution_convert_fusion.2
  4.0 0.0 copy-start.9
  4.0 4.9 %convolution_convert_fusion = bf16[3072,256]{1,0:T(8,128)(2,1)S(1)} fusion(bf16[1024,3072]{1,0:T(8,128)(2,1)} %param.12, bf16[1,256,1024]{2,1,0:T(8,128)(2,1)S(1)} %copy-done.11), kind=kOutput, calls=%fused_computation.2 | convolution fusion | flops 1611399168 | bytes 8388608 | tf_op jit(solution)/shard_map/dot_general | solution.py:172
  8.9 1.2 copy-done.7
  10.1 0.1 multiply_bitcast_fusion.1
  10.2 1.1 pad_maximum_fusion.2
  11.3 10.7 %all-to-all-start = ((bf16[128,16,256]{2,1,0:T(8,128)(2,1)}), bf16[128,16,256]{2,1,0:T(8,128)(2,1)S(1)}, u32[]{:S(2)}, u32[]{:S(2)}) async-start(bf16[128,16,256]{2,1,0:T(8,128)(2,1)} %pad_maximum_fusion.2), calls=%async_computation | async-start | bytes 2097152 | tf_op jit(solution)/shard_map/all_to_all | solution.py:180
  22.0 12.8 %constant_dynamic-slice_fusion = f32[32768,8]{1,0:T(8,128)} fusion(f32[32768,1024]{1,0:T(8,128)} %param.14, s32[]{:T(128)S(6)} %select_n.4), kind=kLoop, calls=%fused_computation.22 | loop fusion | bytes 2097156 | tf_op jit(solution)/shard_map/dynamic_slice | solution.py:182
  34.8 0.8 dynamic_slice.7.skip_ref
  35.6 9.8 %copy.18 = f32[32768,8]{0,1:T(8,128)S(1)} copy(f32[32768,8]{1,0:T(8,128)} %constant_dynamic-slice_fusion) | data formatting | bytes 2097152
  45.3 0.0 all-to-all-done.sig_ref
  45.4 0.0 copy-start.5
  45.4 0.9 copy-done.5
  46.3 0.9 copy-done.6
  47.3 17.1 %channel_convs.1 = (bf16[128,16,256]{2,1,0:T(8,128)(2,1)S(1)}, f32[2048,128]{1,0:T(8,128)}, f32[8,128]{1,0:T(8,128)S(1)}) custom-call(bf16[128,16,256]{2,1,0:T(8,128)(2,1)S(1)} %all-to-all-done.sig_ref, f32[2048,128]{1,0:T(8,128)S(1)} %bitcast.45, f32[8]{0:T(128)S(1)} %dynamic_slice.7.skip_ref, bf16[512,512]{1,0:T(8,128)(2,1)S(1)} %copy-done.3, ...), custom_call_target="tpu_custom_call" | custom-call | flops 10000000000 | bytes 8388608 | tf_op jit(solution)/shard_map/channel_convs/pallas_call | solution.py:141
  64.4 25.7 %all_to_all.15 = bf16[128,16,256]{2,1,0:T(8,128)(2,1)S(1)} all-to-all(bf16[128,16,256]{2,1,0:T(8,128)(2,1)S(1)} %get-tuple-element.8), channel_id=1, replica_groups=mesh['dp'=1,'cp'=128] {'cp'}, dimensions={0} | all-to-all | bytes 2097152 | tf_op jit(solution)/shard_map/all_to_all | solution.py:189
  90.1 0.2 fusion.9
  90.4 0.0 copy-start.13
  90.4 1.8 convolution_bitcast_fusion
  92.2 0.8 fusion.3
  93.0 7.3 %pad_maximum_fusion = f32[1024,4096]{0,1:T(8,128)} fusion(f32[1024,1024]{0,1:T(8,128)S(1)} %fusion.3, f32[1024,3072]{0,1:T(8,128)S(1)} %convolution_bitcast_fusion), kind=kLoop, calls=%fused_computation | loop fusion | flops 4194304 | bytes 33554432 | tf_op jit(solution)/shard_map/concatenate | solution.py:197
  100.3 17.5 %copy.17 = f32[1024,4096]{1,0:T(8,128)} copy(f32[1024,4096]{0,1:T(8,128)} %pad_maximum_fusion) | data formatting | bytes 33554432 | tf_op jit(solution)/shard_map/concatenate | solution.py:197
  117.7 8.8 %all-to-all-start.2 = ((f32[128,8,4096]{2,1,0:T(8,128)}), f32[128,8,4096]{2,1,0:T(8,128)}, u32[]{:S(2)}, u32[]{:S(2)}) async-start(f32[128,8,4096]{2,1,0:T(8,128)} %bitcast.46), calls=%async_computation.2 | async-start | bytes 33554432 | tf_op jit(solution)/shard_map/all_to_all | solution.py:198
  126.6 0.6 reduce_sum.19
  127.2 5.4 %fusion = bf16[1,256,1024]{2,1,0:T(8,128)(2,1)} fusion(bf16[1024,3072]{1,0:T(8,128)(2,1)} %param.12, bf16[1024,256]{1,0:T(8,128)(2,1)S(1)} %get-tuple-element.12, bf16[1024,256]{1,0:T(8,128)(2,1)S(1)} %get-tuple-element.11, bf16[1024,256]{1,0:T(8,128)(2,1)S(1)} %get-tuple-element.15), kind=kOutput, calls=%fused_computation.6 | convolution fusion | flops 1615593472 | bytes 8388608 | tf_op jit(solution)/shard_map/dot_general | solution.py:172
  132.6 245.8 %all-to-all-done.2 = f32[128,8,4096]{2,1,0:T(8,128)} async-done(((f32[128,8,4096]{2,1,0:T(8,128)}), f32[128,8,4096]{2,1,0:T(8,128)}, u32[]{:S(2)}, u32[]{:S(2)}) %all-to-all-start.2) | async-done | bytes 16777248 | tf_op jit(solution)/shard_map/all_to_all | solution.py:198
  378.5 6.7 %reduce_sum.18 = bf16[8,4096]{1,0:T(8,128)(2,1)S(1)} reduce(f32[128,8,4096]{2,1,0:T(8,128)} %all-to-all-done.2, f32[]{:T(128)} %constant.9.clone.1), dimensions={0}, to_apply=%region_0.0 | reduce | flops 4161536 | bytes 16842756 | tf_op jit(solution)/shard_map/reduce_sum | solution.py:199
  385.2 0.6 slice.34
  385.8 0.6 slice.33
  (19 shorter events, 0.0 us)
Async XLA Ops:
  0.6 1.6 copy-start
  0.6 3.4 copy-start.11
  4.0 4.9 %copy-start.9 = (bf16[1024,256]{1,0:T(8,128)(2,1)}, bf16[1024,256]{1,0:T(8,128)(2,1)S(1)}, u32[]{:S(2)}) copy-start(bf16[1024,256]{1,0:T(8,128)(2,1)S(1)} %convolution_convert_fusion.2) | copy-start | bytes 1572868
  8.9 1.2 copy-start.7
  11.3 34.1 %all-to-all-start = ((bf16[128,16,256]{2,1,0:T(8,128)(2,1)}), bf16[128,16,256]{2,1,0:T(8,128)(2,1)S(1)}, u32[]{:S(2)}, u32[]{:S(2)}) async-start(bf16[128,16,256]{2,1,0:T(8,128)(2,1)} %pad_maximum_fusion.2), calls=%async_computation | async-start | bytes 2097152 | tf_op jit(solution)/shard_map/all_to_all | solution.py:180
  35.6 9.8 %copy-start.2 = (bf16[256,1024]{1,0:T(8,128)(2,1)S(1)}, bf16[256,1024]{1,0:T(8,128)(2,1)}, u32[]{:S(2)}) copy-start(bf16[256,1024]{1,0:T(8,128)(2,1)} %constant.25.clone.g1_ref) | copy-start | bytes 1572868
  35.6 9.8 %copy-start.3 = (bf16[512,512]{1,0:T(8,128)(2,1)S(1)}, bf16[512,512]{1,0:T(8,128)(2,1)}, u32[]{:S(2)}) copy-start(bf16[512,512]{1,0:T(8,128)(2,1)} %constant.22.clone.f1_ref) | copy-start | bytes 1572868
  35.6 9.8 %copy-start.4 = (f32[256,256]{1,0:T(8,128)S(1)}, f32[256,256]{1,0:T(8,128)}, u32[]{:S(2)}) copy-start(f32[256,256]{1,0:T(8,128)} %constant.26.clone.tw_ref) | copy-start | bytes 786436
  45.4 1.0 copy-start.5
  46.3 0.9 copy-start.6
  47.3 42.8 %copy-start.8 = (bf16[3072,256]{1,0:T(8,128)(2,1)S(1)}, bf16[3072,256]{1,0:T(8,128)(2,1)}, u32[]{:S(2)}) copy-start(bf16[3072,256]{1,0:T(8,128)(2,1)} %copy-done.7) | copy-start | bytes 4718596
  47.3 42.8 %copy-start.10 = (bf16[1024,256]{1,0:T(8,128)(2,1)S(1)}, bf16[1024,256]{1,0:T(8,128)(2,1)}, u32[]{:S(2)}) copy-start(bf16[1024,256]{1,0:T(8,128)(2,1)} %copy-done.9) | copy-start | bytes 1572868
  64.4 26.0 %copy-start.12 = (bf16[1,256,1024]{2,1,0:T(8,128)(2,1)S(1)}, bf16[1,256,1024]{2,1,0:T(8,128)(2,1)}, u32[]{:S(2)}) copy-start(bf16[1,256,1024]{2,1,0:T(8,128)(2,1)} %param.11) | copy-start | bytes 1572868
  90.4 1.8 copy-start.13
  117.7 260.7 %all-to-all-start.2 = ((f32[128,8,4096]{2,1,0:T(8,128)}), f32[128,8,4096]{2,1,0:T(8,128)}, u32[]{:S(2)}, u32[]{:S(2)}) async-start(f32[128,8,4096]{2,1,0:T(8,128)} %bitcast.46), calls=%async_computation.2 | async-start | bytes 33554432 | tf_op jit(solution)/shard_map/all_to_all | solution.py:198
  378.5 7.9 %copy-start.1 = (bf16[1024,1024]{1,0:T(8,128)(2,1)S(1)}, bf16[1024,1024]{1,0:T(8,128)(2,1)}, u32[]{:S(2)}) copy-start(bf16[1024,1024]{1,0:T(8,128)(2,1)} %param.13) | copy-start | bytes 6291460
where the time goes:
time: 387 us; the launch traced here: 386 us
  waiting for transfers between devices  246 us (64%)
  local copies, waits for them, and re-layouts  46.7 us (12%)
  blocking collectives  25.7 us (7%)
  starting transfers between devices  19.6 us (5%)
  Pallas kernels  17.1 us (4%)
  other arithmetic  16 us (4%)
  matrix products  14.6 us (4%)
    all_to_all x1, waiting for transfers between devices, local_step(): parts = lax.all_to_all(parts, 'cp', 0, 0, tiled=True)  246 us
    all_to_all x1, blocking collectives, local_step(): res = lax.all_to_all(res, 'cp', 0, 0, tiled=True)  25.7 us
    concatenate x1, local copies, waits for them, and re-layouts, local_step(): jnp.concatenate([dw_in, dw_out], axis=1)  17.5 us
    pallas_call x1, Pallas kernels, channel_convs(): pl.pallas_call(functools.partial(conv_kernel, n_chans), out_shape=(jax.Sh...  17.1 us
    dot_general x5, matrix products, mm(): lax.dot_general(a, b, (((ca,), (cb,)), ((), ())), preferred_element_type=...  14.6 us
    unnamed x29, local copies, waits for them, and re-layouts  14.4 us
    dynamic_slice x1, local copies, waits for them, and re-layouts, local_step(): taps = lax.dynamic_slice_in_dim(filt_taps, rank * n_chans, n_chans, axis=1)  12.8 us
    all_to_all x1, starting transfers between devices, local_step(): sig = lax.all_to_all(sig, 'cp', 0, 0, tiled=True)  10.7 us
  transfers between devices with their start and end apart: 2, of which 1 were waited for; matrix products, arithmetic and copies ran while one was open for 8% of the time, Pallas kernels for 0%

commit v1 on v0

--- a/solution.py
+++ b/solution.py
@@ -157,6 +157,228 @@
     )(sig, taps, skip, *[jnp.asarray(tab) for tab in tables])
 
 
+RING = 4
+PART_ORDERS = ((0, 1, 2), (1, 2, 0), (2, 0, 1))
+
+
+def part_columns(total):
+    tiles = total // 128
+    ends = [0, (tiles + 2) // 3 * 128, ((tiles + 2) // 3 + (tiles + 1) // 3) * 128, total]
+    return [(ends[i], ends[i + 1]) for i in range(3)]
+
+
+def grad_kernel(n_in, x_ref, z_ref, d_ref, do_ref, win_ref, wout_ref, *scratch):
+    (x_peer, z_peer, d_peer, do_peer, p0, p1, p2, via0, via1, via2, fin0, fin1, fin2, r10, r11, r12,
+     via20, via21, via22, fin20, fin21, fin22, r20, r21, r22, via30, via31, via32, fin30, fin31, fin32,
+     send_sem, recv_sem, swap_send, swap_recv) = scratch
+    partial = (p0, p1, p2)
+    vias = ((via0, via1, via2), (via20, via21, via22), (via30, via31, via32))
+    fins = ((fin0, fin1, fin2), (fin20, fin21, fin22), (fin30, fin31, fin32))
+    reds = ((r10, r11, r12), (r20, r21, r22))
+    rank = lax.axis_index("cp")
+    core = lax.rem(rank, 2)
+    chip = lax.div(rank, 2)
+    coords = (lax.div(chip, 16), lax.rem(lax.div(chip, 4), 4), lax.rem(chip, 4))
+    strides = (32, 8, 2)
+    peer = rank + 1 - 2 * core
+    n_out = do_ref.shape[1]
+    cols = part_columns(n_in + n_out)
+
+    def at_offset(dim, step):
+        pos = lax.rem(coords[dim] + step, RING)
+        return pos, rank + (pos - coords[dim]) * strides[dim]
+
+    nxt = [at_offset(dim, 1) for dim in range(3)]
+    opp = [at_offset(dim, 2) for dim in range(3)]
+    prv = [at_offset(dim, 3) for dim in range(3)]
+
+    barrier = pltpu.get_barrier_semaphore()
+    for device in [peer] + [spot[1] for spot in nxt] + [spot[1] for spot in prv]:
+        pl.semaphore_signal(barrier, inc=1, device_id={"cp": device}, device_id_type=pl.DeviceIdType.MESH)
+    pl.semaphore_wait(barrier, 7)
+
+    def remote(src, dst, send, recv, device):
+        return pltpu.make_async_remote_copy(src_ref=src, dst_ref=dst, send_sem=send, recv_sem=recv,
+                                            device_id={"cp": device}, device_id_type=pl.DeviceIdType.MESH)
+
+    swaps = []
+
+    def swap(src, dst):
+        copy = remote(src, dst, swap_send.at[len(swaps)], swap_recv.at[len(swaps)], peer)
+        copy.start()
+        swaps.append(copy)
+
+    swap(x_ref.at[:, 1 - core], x_peer)
+    row_ranges = [(lo, min(hi, n_in)) for lo, hi in cols]
+    for lo, hi in row_ranges:
+        swap(d_ref.at[pl.ds(lo, hi - lo)], d_peer.at[pl.ds(lo, hi - lo)])
+    swap(z_ref.at[:, 1 - core], z_peer)
+    swap(do_ref, do_peer)
+
+    n_tok = x_ref.shape[-1]
+    n_rows = x_ref.shape[0] * x_ref.shape[2]
+
+    def flat(val):
+        return val.reshape(n_rows, n_tok)
+
+    def mm(a, b, cb):
+        return lax.dot_general(a, b, (((1,), (cb,)), ((), ())), preferred_element_type=F32)
+
+    def put(part, col, val):
+        partial[part][:, :, :, :, pl.ds(col, val.shape[1])] = val.reshape(
+            RING, RING, RING, x_ref.shape[2], val.shape[1])
+
+    def slab(ref, axis, pos, col=None):
+        index = [slice(None)] * len(ref.shape)
+        if axis is not None:
+            index[axis] = pos
+        if col is not None:
+            index[-1] = pl.ds(*col)
+        return ref.at[tuple(index)]
+
+    copies = {}
+
+    def send(part, phase, which, src, dst, device):
+        slot = (phase * 3 + part) * 6 + which
+        copy = remote(src, dst, send_sem.at[slot], recv_sem.at[slot], device)
+        copy.start()
+        copies[part, phase, which] = copy
+
+    def source(part, phase):
+        return partial[part] if phase == 0 else reds[phase - 1][part]
+
+    def axis_of(part, phase):
+        order = PART_ORDERS[part]
+        left = sorted(order[phase:])
+        return left.index(order[phase])
+
+    def split(part):
+        lo, hi = cols[part]
+        first = ((hi - lo) // 128 + 1) // 2 * 128
+        return (0, first), (first, hi - lo - first)
+
+    def launch(part, phase):
+        dim, axis, src = PART_ORDERS[part][phase], axis_of(part, phase), source(part, phase)
+        a_cols, b_cols = split(part)
+        via, fin = vias[phase][part], fins[phase][part]
+        send(part, phase, 0, slab(src, axis, opp[dim][0], a_cols), slab(via, None, None, a_cols), nxt[dim][1])
+        send(part, phase, 1, slab(src, axis, opp[dim][0], b_cols), slab(via, None, None, b_cols), prv[dim][1])
+        send(part, phase, 2, slab(src, axis, nxt[dim][0], b_cols), slab(fin, 0, 0, b_cols), nxt[dim][1])
+        send(part, phase, 3, slab(src, axis, prv[dim][0], a_cols), slab(fin, 0, 1, a_cols), prv[dim][1])
+
+    def each_block(shape, body):
+        lead = shape[:-2]
+        count = int(np.prod(lead)) if lead else 1
+        if count == 1:
+            body(tuple(0 for _ in lead))
+            return
+
+        def step(i, carry):
+            index = []
+            for size in reversed(lead):
+                index.insert(0, lax.rem(i, size))
+                i = lax.div(i, size)
+            body(tuple(index))
+            return carry
+
+        lax.fori_loop(0, count, step, 0, unroll=min(count, 4))
+
+    def relay(part, phase):
+        dim, axis, src = PART_ORDERS[part][phase], axis_of(part, phase), source(part, phase)
+        a_cols, b_cols = split(part)
+        via, fin = vias[phase][part], fins[phase][part]
+        for which, col, spot, side in ((0, a_cols, nxt[dim], 0), (1, b_cols, prv[dim], 1)):
+            copies[part, phase, which].wait_recv()
+            span = pl.ds(*col)
+
+            def add(index):
+                at = index[:axis] + (spot[0],) + index[axis:]
+                src[at + (slice(None), span)] = src[at + (slice(None), span)] + via[index + (slice(None), span)]
+
+            each_block(via.shape, add)
+            send(part, phase, 4 + which, slab(src, axis, spot[0], col), slab(fin, 0, side, col), spot[1])
+
+    def finish(part, phase):
+        dim, axis, src = PART_ORDERS[part][phase], axis_of(part, phase), source(part, phase)
+        via, fin = vias[phase][part], fins[phase][part]
+        for which in range(2, 6):
+            copies[part, phase, which].wait_recv()
+
+        def add(index):
+            at = index[:axis] + (coords[dim],) + index[axis:]
+            total = src[at] + fin[(0,) + index] + fin[(1,) + index]
+            if phase < 2:
+                reds[phase][part][index] = total
+            else:
+                lo, hi = cols[part]
+                mid = min(max(n_in, lo), hi)
+                if mid > lo:
+                    win_ref[:, lo:mid] = total[:, :mid - lo].astype(win_ref.dtype)
+                if hi > mid:
+                    wout_ref[:, mid - n_in:hi - n_in] = total[:, mid - lo:].astype(wout_ref.dtype)
+
+        each_block(via.shape, add)
+
+    x_own = flat(x_ref[:, core])
+    swaps[0].wait_recv()
+    x_other = flat(x_peer[...])
+    for part in range(3):
+        lo, hi = cols[part]
+        swaps[1 + part].wait_recv()
+        for start in range(lo, min(hi, n_in), 512):
+            size = min(512, min(hi, n_in) - start)
+            put(part, start - lo, mm(x_own, d_ref[pl.ds(start, size), :], 1)
+                + mm(x_other, d_peer[pl.ds(start, size), :], 1))
+        if hi > n_in:
+            swaps[4].wait_recv()
+            swaps[5].wait_recv()
+            z_own, z_other = flat(z_ref[:, core]), flat(z_peer[...])
+            for start in range(max(lo, n_in), hi, 512):
+                size = min(512, hi - start)
+                put(part, start - lo, mm(z_own, do_ref[:, pl.ds(start - n_in, size)], 0)
+                    + mm(z_other, do_peer[:, pl.ds(start - n_in, size)], 0))
+        launch(part, 0)
+    for phase in range(3):
+        for part in range(3):
+            relay(part, phase)
+        for part in range(3):
+            finish(part, phase)
+            if phase < 2:
+                launch(part, phase + 1)
+    for copy in copies.values():
+        copy.wait_send()
+    for copy in swaps:
+        copy.wait_send()
+
+
+def weight_grads(x_cm, z_cm, d_cm, d_out):
+    n_chip, n_core, n_row, n_tok = x_cm.shape
+    n_in, n_out = d_cm.shape[0], d_out.shape[1]
+    widths = [hi - lo for lo, hi in part_columns(n_in + n_out)]
+    vmem = pl.BlockSpec(memory_space=pltpu.VMEM)
+    scratch = [pltpu.VMEM((n_chip, n_row, n_tok), BF16), pltpu.VMEM((n_chip, n_row, n_tok), BF16),
+               pltpu.VMEM(d_cm.shape, BF16), pltpu.VMEM(d_out.shape, BF16)]
+    scratch += [pltpu.VMEM((RING,) * 3 + (n_row, w), F32) for w in widths]
+    for n_lead in (2, 1, 0):
+        lead = (RING,) * n_lead
+        scratch += [pltpu.VMEM(lead + (n_row, w), F32) for w in widths]
+        scratch += [pltpu.VMEM((2,) + lead + (n_row, w), F32) for w in widths]
+        if n_lead:
+            scratch += [pltpu.VMEM(lead + (n_row, w), F32) for w in widths]
+    scratch += [pltpu.SemaphoreType.DMA((54,)), pltpu.SemaphoreType.DMA((54,)),
+                pltpu.SemaphoreType.DMA((6,)), pltpu.SemaphoreType.DMA((6,))]
+    return pl.pallas_call(
+        functools.partial(grad_kernel, n_in),
+        out_shape=(jax.ShapeDtypeStruct((n_row, n_in), BF16), jax.ShapeDtypeStruct((n_row, n_out), BF16)),
+        in_specs=[vmem] * 4,
+        out_specs=(vmem, vmem),
+        scratch_shapes=scratch,
+        compiler_params=pltpu.CompilerParams(vmem_limit_bytes=56 * 2 ** 20, collective_id=0, has_side_effects=True),
+        cost_estimate=pl.CostEstimate(flops=5 * 10 ** 9, bytes_accessed=8 * 2 ** 20, transcendentals=0),
+        name="weight_grads",
+    )(x_cm, z_cm, d_cm, d_out)
+
+
 def solution(mesh):
     ctx_size = mesh.shape["cp"]
 
@@ -192,12 +414,10 @@
         z_act = q_act * y_act
         d_qkv = jnp.concatenate([dz_act * y_act, du_act * v_act, du_act * k_act], axis=0)
         grad_x = mm(d_qkv, w_in, 0, 1).astype(BF16)[None]
-        dw_in = mm(x_tok, d_qkv, 0, 1)
-        dw_out = mm(z_act, do_tok, 1, 0)
-        parts = jnp.concatenate([dw_in, dw_out], axis=1).reshape(ctx_size, n_chans, 4 * width)
-        parts = lax.all_to_all(parts, "cp", 0, 0, tiled=True)
-        sums = jnp.sum(parts, axis=0).astype(BF16)
-        return grad_x, sums[:, :3 * width], sums[:, 3 * width:], grad_filt, grad_skip
+        by_core = (ctx_size // 2, 2, n_chans, n_tok)
+        grad_w_in, grad_w_out = weight_grads(
+            x_tok.T.reshape(by_core), z_act.reshape(by_core), d_qkv, do_tok)
+        return grad_x, grad_w_in, grad_w_out, grad_filt, grad_skip
 
     seq_spec = P("dp", "cp", None)
     row_spec = P(("dp", "cp"), None)

time: 387 us -> 158 us (0.41)
  the two profiles are of different devices: /device:TPU:11 before, /device:TPU:0 now
where the time goes in v1:
time: 158 us; the launch traced here: 157 us
  Pallas kernels  67.9 us (43%)
  local copies, waits for them, and re-layouts  33.7 us (21%)
  starting transfers between devices  21.6 us (14%)
  waiting for transfers between devices  16.1 us (10%)
  matrix products  11.2 us (7%)
  other arithmetic  5.64 us (4%)
    pallas_call x1, Pallas kernels, weight_grads(): pl.pallas_call(functools.partial(grad_kernel, n_in), out_shape=(jax.Shape...  50 us
    unnamed x23, local copies, waits for them, and re-layouts  18.1 us
    pallas_call x1, Pallas kernels, channel_convs(): pl.pallas_call(functools.partial(conv_kernel, n_chans), out_shape=(jax.Sh...  17.9 us
    all_to_all x1, waiting for transfers between devices, local_step(): res = lax.all_to_all(res, 'cp', 0, 0, tiled=True)  16.1 us
    dynamic_slice x1, local copies, waits for them, and re-layouts, local_step(): taps = lax.dynamic_slice_in_dim(filt_taps, rank * n_chans, n_chans, axis=1)  12.8 us
    all_to_all x1, starting transfers between devices, local_step(): sig = lax.all_to_all(sig, 'cp', 0, 0, tiled=True)  11.7 us
    dot_general x3, matrix products, mm(): lax.dot_general(a, b, (((ca,), (cb,)), ((), ())), preferred_element_type=...  11.2 us
    all_to_all x1, starting transfers between devices, local_step(): res = lax.all_to_all(res, 'cp', 0, 0, tiled=True)  9.87 us
  transfers between devices with their start and end apart: 2, of which 1 were waited for; matrix products, arithmetic and copies ran while one was open for 17% of the time, Pallas kernels for 0%

profile of v1, /device:TPU:0, one launch (start us, length us, event | category | flops | bytes accessed | tf_op | source)
XLA Modules:
  0.0 156.8 jit_solution(9466337071869868548)
XLA Ops:
  0.6 0.0 copy-start
  0.6 0.0 copy-start.9
  0.7 4.9 %convolution_convert_fusion = bf16[3072,256]{1,0:T(8,128)(2,1)S(1)} fusion(bf16[1024,3072]{1,0:T(8,128)(2,1)} %param.12, bf16[1,256,1024]{2,1,0:T(8,128)(2,1)} %param.11), kind=kOutput, calls=%fused_computation | convolution fusion | flops 1611399168 | bytes 8388608 | tf_op jit(solution)/shard_map/dot_general | solution.py:394
  5.6 0.0 copy-done
  5.6 0.0 copy-done.9
  5.6 0.7 convolution_convert_fusion.2
  6.4 0.0 copy-start.8
  6.4 0.1 multiply_bitcast_fusion.1
  6.5 0.3 copy-done.7
  6.8 0.4 copy-done.8
  7.1 1.1 pad_maximum_fusion.1
  8.2 11.7 %all-to-all-start = ((bf16[128,16,256]{2,1,0:T(8,128)(2,1)}), bf16[128,16,256]{2,1,0:T(8,128)(2,1)}, u32[]{:S(2)}, u32[]{:S(2)}) async-start(bf16[128,16,256]{2,1,0:T(8,128)(2,1)} %pad_maximum_fusion.1), calls=%async_computation | async-start | bytes 2097152 | tf_op jit(solution)/shard_map/all_to_all | solution.py:402
  20.0 12.8 %constant_dynamic-slice_fusion = f32[32768,8]{1,0:T(8,128)} fusion(f32[32768,1024]{1,0:T(8,128)} %param.14, s32[]{:T(128)S(6)} %select_n.4), kind=kLoop, calls=%fused_computation.15 | loop fusion | bytes 2097156 | tf_op jit(solution)/shard_map/dynamic_slice | solution.py:404
  32.8 9.7 %copy.19 = f32[32768,8]{0,1:T(8,128)S(1)} copy(f32[32768,8]{1,0:T(8,128)} %constant_dynamic-slice_fusion) | data formatting | bytes 2097152
  42.5 0.8 dynamic_slice.7.skip_ref
  43.3 0.0 all-to-all-done.sig_ref
  43.3 1.0 copy-done.2
  44.3 1.0 copy-done.3
  45.4 0.9 copy-done.5
  46.3 0.9 copy-done.6
  47.3 17.9 %channel_convs.1 = (bf16[128,16,256]{2,1,0:T(8,128)(2,1)S(1)}, f32[2048,128]{1,0:T(8,128)}, f32[8,128]{1,0:T(8,128)S(1)}) custom-call(bf16[128,16,256]{2,1,0:T(8,128)(2,1)} %all-to-all-done.sig_ref, f32[2048,128]{1,0:T(8,128)S(1)} %bitcast.41, f32[8]{0:T(128)S(1)} %dynamic_slice.7.skip_ref, bf16[512,512]{1,0:T(8,128)(2,1)S(1)} %copy-done.2, ...), custom_call_target="tpu_custom_call" | custom-call | flops 10000000000 | bytes 8388608 | tf_op jit(solution)/shard_map/channel_convs/pallas_call | solution.py:141
  65.1 1.0 copy-done.1
  66.1 9.9 %all-to-all-start.1 = ((bf16[128,16,256]{2,1,0:T(8,128)(2,1)}), bf16[128,16,256]{2,1,0:T(8,128)(2,1)S(1)}, u32[]{:S(2)}, u32[]{:S(2)}) async-start(bf16[128,16,256]{2,1,0:T(8,128)(2,1)} %copy-done.1), calls=%async_computation.1 | async-start | bytes 2097152 | tf_op jit(solution)/shard_map/all_to_all | solution.py:411
  76.0 2.1 %copy.18 = bf16[1024,256]{1,0:T(8,128)(2,1)} copy(bf16[1024,256]{0,1:T(8,128)(2,1)} %bitcast.43) | data formatting | bytes 1048576 | tf_op jit(solution)/shard_map/transpose | solution.py:419
  78.1 0.6 reduce_sum.9
  78.7 16.1 %all-to-all-done.1 = bf16[128,16,256]{2,1,0:T(8,128)(2,1)S(1)} async-done(((bf16[128,16,256]{2,1,0:T(8,128)(2,1)}), bf16[128,16,256]{2,1,0:T(8,128)(2,1)S(1)}, u32[]{:S(2)}, u32[]{:S(2)}) %all-to-all-start.1) | async-done | bytes 1048608 | tf_op jit(solution)/shard_map/all_to_all | solution.py:411
  94.7 2.6 %fusion.2 = (bf16[1024,256]{1,0:T(8,128)(2,1)}, bf16[1024,256]{1,0:T(8,128)(2,1)S(1)}, bf16[1024,256]{1,0:T(8,128)(2,1)S(1)}, bf16[1024,256]{1,0:T(8,128)(2,1)S(1)}) fusion(bf16[128,16,256]{2,1,0:T(8,128)(2,1)S(1)} %all-to-all-done.1, bf16[3072,256]{1,0:T(8,128)(2,1)} %copy-done.7, bf16[1024,256]{1,0:T(8,128)(2,1)} %copy-done.8), kind=kLoop, calls=%fused_computation.11 | loop fusion | flops 1048576 | bytes 5242880 | tf_op jit(solution)/shard_map/mul | solution.py:414
  97.3 1.3 pad_maximum_fusion.d_ref
  98.6 5.5 %fusion = bf16[1,256,1024]{2,1,0:T(8,128)(2,1)} fusion(bf16[1024,3072]{1,0:T(8,128)(2,1)} %param.12, bf16[1024,256]{1,0:T(8,128)(2,1)S(1)} %get-tuple-element.16, bf16[1024,256]{1,0:T(8,128)(2,1)S(1)} %get-tuple-element.17, bf16[1024,256]{1,0:T(8,128)(2,1)S(1)} %get-tuple-element.20), kind=kOutput, calls=%fused_computation.4 | convolution fusion | flops 1615593472 | bytes 8388608 | tf_op jit(solution)/shard_map/dot_general | solution.py:394
  104.1 50.0 %weight_grads.1 = (bf16[8,3072]{1,0:T(8,128)(2,1)}, bf16[8,1024]{1,0:T(8,128)(2,1)}) custom-call(bf16[64,2,8,256]{3,2,1,0:T(8,128)(2,1)} %bitcast.44, bf16[64,2,8,256]{3,2,1,0:T(8,128)(2,1)} %bitcast.42, bf16[3072,256]{1,0:T(8,128)(2,1)} %pad_maximum_fusion.d_ref, bf16[256,1024]{1,0:T(8,128)(2,1)} %bitcast.45), custom_call_target="tpu_custom_call" | custom-call | flops 5000000000 | bytes 8388608 | tf_op jit(solution)/shard_map/weight_grads/pallas_call | solution.py:370
  154.1 1.4 copy.22
  155.5 1.3 copy.23
  (8 shorter events, 0.0 us)
Async XLA Ops:
  0.6 4.9 %copy-start = (bf16[1024,1024]{1,0:T(8,128)(2,1)S(1)}, bf16[1024,1024]{1,0:T(8,128)(2,1)}, u32[]{:S(2)}) copy-start(bf16[1024,1024]{1,0:T(8,128)(2,1)} %param.13) | copy-start | bytes 6291460
  0.6 4.9 %copy-start.9 = (bf16[1,256,1024]{2,1,0:T(8,128)(2,1)S(1)}, bf16[1,256,1024]{2,1,0:T(8,128)(2,1)}, u32[]{:S(2)}) copy-start(bf16[1,256,1024]{2,1,0:T(8,128)(2,1)} %param.16) | copy-start | bytes 1572868
  5.6 1.2 copy-start.7
  6.4 0.8 copy-start.8
  8.2 35.1 %all-to-all-start = ((bf16[128,16,256]{2,1,0:T(8,128)(2,1)}), bf16[128,16,256]{2,1,0:T(8,128)(2,1)}, u32[]{:S(2)}, u32[]{:S(2)}) async-start(bf16[128,16,256]{2,1,0:T(8,128)(2,1)} %pad_maximum_fusion.1), calls=%async_computation | async-start | bytes 2097152 | tf_op jit(solution)/shard_map/all_to_all | solution.py:402
  32.8 10.5 %copy-start.4 = (bf16[512,256]{1,0:T(8,128)(2,1)S(1)}, bf16[512,256]{1,0:T(8,128)(2,1)}, u32[]{:S(2)}) copy-start(bf16[512,256]{1,0:T(8,128)(2,1)} %constant.23.clone.f2_ref) | copy-start | bytes 786436
  43.3 1.0 copy-start.2
  44.3 1.0 copy-start.3
  45.4 0.9 copy-start.5
  46.3 0.9 copy-start.6
  65.1 1.0 copy-start.1
  66.1 28.6 %all-to-all-start.1 = ((bf16[128,16,256]{2,1,0:T(8,128)(2,1)}), bf16[128,16,256]{2,1,0:T(8,128)(2,1)S(1)}, u32[]{:S(2)}, u32[]{:S(2)}) async-start(bf16[128,16,256]{2,1,0:T(8,128)(2,1)} %copy-done.1), calls=%async_computation.1 | async-start | bytes 2097152 | tf_op jit(solution)/shard_map/all_to_all | solution.py:411

commit v2 on v1

--- a/solution.py
+++ b/solution.py
@@ -55,41 +55,100 @@
     return hi, lo
 
 
-def conv_kernel(n_chans, sig_ref, filt_ref, skip_ref, f1_ref, f2_ref, g2_ref, g1_ref, tw_ref,
-                out_ref, gfilt_ref, gskip_ref, sig_f32, out_f32):
-    n_src = sig_ref.shape[0]
-    n_rows, n_lanes = 2 * n_src, sig_ref.shape[2] // 2
-    for half in range(2):
-        sig_f32[half] = sig_ref[:, :, half * n_lanes:(half + 1) * n_lanes].astype(F32).reshape(sig_f32.shape[1:])
-
-    def rows_of(chan):
-        val = jnp.concatenate([sig_f32[0, pl.ds(chan, n_src, stride=2 * n_chans), :],
-                               sig_f32[1, pl.ds(chan, n_src, stride=2 * n_chans), :]], axis=0)
-        return val
-
-    def taps_of(chan):
-        return jnp.concatenate([filt_ref[pl.ds(chan, n_src, stride=2 * n_chans), :],
-                                filt_ref[pl.ds(n_chans + chan, n_src, stride=2 * n_chans), :]], axis=0)
-
-    wr, wi = tw_ref[:, :n_lanes], tw_ref[:, n_lanes:]
-    f1h, f1l = f1_ref[:, :n_rows], f1_ref[:, n_rows:]
-    f2h, f2l = f2_ref[:2 * n_lanes], f2_ref[2 * n_lanes:]
-    g2h, g2l = g2_ref[:2 * n_lanes], g2_ref[2 * n_lanes:]
-    g1h, g1l = g1_ref[:, :2 * n_rows], g1_ref[:, 2 * n_rows:]
+def mix_kernel(u_ref, dy_ref, filt_ref, skip_ref, f1_hbm, f2_hbm, g2_hbm, g1_hbm, tw_hbm,
+               y_ref, du_ref, gfilt_ref, gskip_ref,
+               u_in, dy_in, y_out, du_out, u_f32, dy_f32, out_f32, wide, flip, taps, u_spec, h_spec, d_spec,
+               f1_ref, f2_ref, g2_ref, g1_ref, tw_ref, load_sem, wide_sem, send_sem, recv_sem):
+    n_dev, n_chans, n_tok = u_ref.shape
+    n_lanes = n_tok // 2
+    n_rows = 2 * n_dev
+    n_pairs = n_chans // 2
+    rank = lax.axis_index("cp")
+
+    loads = [pltpu.make_async_copy(src, dst, load_sem.at[i]) for i, (src, dst) in enumerate(
+        ((f1_hbm, f1_ref), (f2_hbm, f2_ref), (g2_hbm, g2_ref), (g1_hbm, g1_ref), (tw_hbm, tw_ref)))]
+    n_wide = wide.shape[0]
+    first_lane = pl.multiple_of(lax.div(rank * n_chans, 128) * 128, 128)
+    wides = [pltpu.make_async_copy(
+        filt_ref.at[pl.ds(i * wide.shape[1], wide.shape[1]), pl.ds(first_lane, 128)], wide.at[i], wide_sem.at[i])
+        for i in range(n_wide)]
+
+    def others(body):
+        def step(i, carry):
+            body(lax.rem(rank + i, n_dev))
+            return carry
+
+        lax.fori_loop(1, n_dev, step, 0)
+
+    barrier = pltpu.get_barrier_semaphore()
+    others(lambda dev: pl.semaphore_signal(barrier, inc=1, device_id={"cp": dev}, device_id_type=pl.DeviceIdType.MESH))
+    for copy in wides + loads:
+        copy.start()
+    pl.semaphore_wait(barrier, n_dev - 1)
+
+    def exchange(which, src, dst):
+        def send(dev):
+            pltpu.make_async_remote_copy(
+                src_ref=src.at[dev], dst_ref=dst.at[rank], send_sem=send_sem.at[which], recv_sem=recv_sem.at[which],
+                device_id={"cp": dev}, device_id_type=pl.DeviceIdType.MESH).start()
+
+        others(send)
+        dst[rank] = src[rank]
+
+    def wait_all(sem, which, ref):
+        part = ref.at[pl.ds(0, n_dev - 1)]
+        pltpu.make_async_copy(part, part, sem.at[which]).wait()
+
+    exchange(0, u_ref, u_in)
+    exchange(1, dy_ref, dy_in)
+
+    own_row = pl.multiple_of(lax.rem(rank * n_chans, 128), n_chans)
+    per_wide = wide.shape[1] // n_lanes
+
+    for i in range(n_wide):
+        wides[i].wait()
+
+        def turn(j, carry):
+            for k in range(4):
+                tile = 4 * j + k
+                flip[k] = wide[i, pl.ds(pl.multiple_of(tile * n_lanes, n_lanes), n_lanes), :].T
+                at = pl.multiple_of((i * per_wide + tile) * n_chans, n_chans)
+                taps[pl.ds(at, n_chans), :] = flip[k, pl.ds(own_row, n_chans), :]
+            return carry
+
+        lax.fori_loop(0, per_wide // 4, turn, 0)
+    for copy in loads:
+        copy.wait()
+
+    def f1(i):
+        return f1_ref[:, i * n_rows:(i + 1) * n_rows]
+
+    def g1(i):
+        return g1_ref[:, 2 * i * n_rows:2 * (i + 1) * n_rows]
+
+    def f2(i):
+        return f2_ref[2 * i * n_lanes:2 * (i + 1) * n_lanes]
+
+    def g2(i):
+        return g2_ref[2 * i * n_lanes:2 * (i + 1) * n_lanes]
+
+    def twist():
+        return tw_ref[:, :n_lanes], tw_ref[:, n_lanes:]
 
     def second(stage):
+        wr, wi = twist()
         parts = []
         for i in range(2):
             ar = stage[:n_rows, i * n_lanes:(i + 1) * n_lanes]
             ai = stage[n_rows:, i * n_lanes:(i + 1) * n_lanes]
             parts.append(jnp.concatenate([ar * wr - ai * wi, ar * wi + ai * wr], axis=1))
         bh, bl = halves(jnp.concatenate(parts, axis=0))
-        spec = dot(bh, f2h) + (dot(bh, f2l) + dot(bl, f2h))
-        return spec[:, :n_lanes], spec[:, n_lanes:]
+        return dot(bh, f2(0)) + (dot(bh, f2(1)) + dot(bl, f2(0)))
 
     def inverse(pr, pi):
+        wr, wi = twist()
         ph, pll = halves(jnp.concatenate([pr, pi], axis=1))
-        mid = dot(ph, g2h) + (dot(ph, g2l) + dot(pll, g2h))
+        mid = dot(ph, g2(0)) + (dot(ph, g2(1)) + dot(pll, g2(0)))
         tr, ti = [], []
         for i in range(2):
             gr = mid[i * n_rows:(i + 1) * n_rows, :n_lanes]
@@ -97,64 +156,130 @@
             tr.append(gr * wr + gi * wi)
             ti.append(gi * wr - gr * wi)
         th, tl = halves(jnp.concatenate([jnp.concatenate(tr, axis=1), jnp.concatenate(ti, axis=1)], axis=0))
-        return dot(g1h, th) + (dot(g1h, tl) + dot(g1l, th))
-
-    def pair(step, carry):
-        c0 = 2 * step
-        u_val = jnp.concatenate([rows_of(c0), rows_of(c0 + 1)], axis=1)
-        dy_val = jnp.concatenate([rows_of(n_chans + c0), rows_of(n_chans + c0 + 1)], axis=1)
-        h_val = jnp.concatenate([taps_of(c0), taps_of(c0 + 1)], axis=1)
-        u_bf, dy_bf = u_val.astype(BF16), dy_val.astype(BF16)
-        h_hi, h_lo = halves(h_val)
-        ur, ui = second(dot(f1h, u_bf) + dot(f1l, u_bf))
-        dr, di = second(dot(f1h, dy_bf) + dot(f1l, dy_bf))
-        hr, hi = second(dot(f1h, h_hi) + (dot(f1h, h_lo) + dot(f1l, h_hi)))
-        y_lin = inverse(ur * hr - ui * hi, ur * hi + ui * hr)
-        du_lin = inverse(dr * hr + di * hi, di * hr - dr * hi)
-        gh_lin = inverse(dr * ur + di * ui, di * ur - dr * ui)
+        return dot(g1(0), th) + (dot(g1(0), tl) + dot(g1(1), th))
+
+    def pairs(body):
+        def step(p, carry):
+            body(p)
+            return carry
+
+        lax.fori_loop(0, n_pairs, step, 0)
+
+    def rows_of(ref, chan):
+        return jnp.concatenate([ref[0, pl.ds(chan, n_dev, stride=n_chans), :],
+                                ref[1, pl.ds(chan, n_dev, stride=n_chans), :]], axis=0)
+
+    def both(ref, p):
+        return jnp.concatenate([rows_of(ref, 2 * p), rows_of(ref, 2 * p + 1)], axis=1)
+
+    def widen(src, dst):
+        for half in range(2):
+            dst[half] = src[:, :, half * n_lanes:(half + 1) * n_lanes].astype(F32).reshape(dst.shape[1:])
+
+    def parts_of(ref, p):
+        return ref[p, :, :n_lanes], ref[p, :, n_lanes:]
+
+    def taps_spec(p):
+        def one(chan):
+            return jnp.concatenate([taps[pl.ds(chan, n_dev, stride=2 * n_chans), :],
+                                    taps[pl.ds(n_chans + chan, n_dev, stride=2 * n_chans), :]], axis=0)
+
+        h_hi, h_lo = halves(jnp.concatenate([one(2 * p), one(2 * p + 1)], axis=1))
+        h_spec[p] = second(dot(f1(0), h_hi) + (dot(f1(0), h_lo) + dot(f1(1), h_hi)))
+
+    pairs(taps_spec)
+
+    def filtered(sig, spec, sign):
+        def one(p):
+            val = both(sig, p)
+            low = val.astype(BF16)
+            spec[p] = second(dot(f1(0), low) + dot(f1(1), low))
+            sr, si = parts_of(spec, p)
+            hr, hi = parts_of(h_spec, p)
+            if sign > 0:
+                lin = inverse(sr * hr - si * hi, sr * hi + si * hr)
+            else:
+                lin = inverse(sr * hr + si * hi, si * hr - sr * hi)
+            for i in range(2):
+                chan = 2 * p + i
+                cols = slice(i * n_lanes, (i + 1) * n_lanes)
+                res = lin[:, cols] + skip_ref[rank * n_chans + chan] * val[:, cols]
+                for odd in range(2):
+                    out_f32[odd, pl.ds(chan, n_dev, stride=n_chans), :] = res[odd * n_dev:(odd + 1) * n_dev]
+
+        pairs(one)
+
+    def narrow(dst):
+        for half in range(2):
+            dst[:, :, half * n_lanes:(half + 1) * n_lanes] = out_f32[half].astype(BF16).reshape(
+                n_dev, n_chans, n_lanes)
+
+    wait_all(recv_sem, 0, u_in)
+    widen(u_in, u_f32)
+    filtered(u_f32, u_spec, 1)
+    narrow(y_out)
+    exchange(2, y_out, y_ref)
+    wait_all(recv_sem, 1, dy_in)
+    widen(dy_in, dy_f32)
+    filtered(dy_f32, d_spec, -1)
+    narrow(du_out)
+    exchange(3, du_out, du_ref)
+
+    def taps_grad(p):
+        ur, ui = parts_of(u_spec, p)
+        dr, di = parts_of(d_spec, p)
+        lin = inverse(dr * ur + di * ui, di * ur - dr * ui)
+        prod = both(u_f32, p) * both(dy_f32, p)
         for i in range(2):
-            chan = c0 + i
+            chan = 2 * p + i
             cols = slice(i * n_lanes, (i + 1) * n_lanes)
-            skip = skip_ref[chan]
-            y_out = (y_lin[:, cols] + skip * u_val[:, cols]).astype(BF16).astype(F32)
-            du_out = (du_lin[:, cols] + skip * dy_val[:, cols]).astype(BF16).astype(F32)
-            gskip_ref[pl.ds(chan, 1), :] = jnp.sum(u_val[:, cols] * dy_val[:, cols], axis=0, keepdims=True)
+            gskip_ref[pl.ds(chan, 1), :] = jnp.sum(prod[:, cols], axis=0, keepdims=True)
             for odd in range(2):
-                rows = slice(odd * n_src, (odd + 1) * n_src)
-                out_f32[odd, pl.ds(chan, n_src, stride=2 * n_chans), :] = y_out[rows]
-                out_f32[odd, pl.ds(n_chans + chan, n_src, stride=2 * n_chans), :] = du_out[rows]
-                gfilt_ref[pl.ds(odd * n_chans + chan, n_src, stride=2 * n_chans), :] = gh_lin[rows, cols]
-        return carry
-
-    lax.fori_loop(0, n_chans // 2, pair, 0)
-    for half in range(2):
-        out_ref[:, :, half * n_lanes:(half + 1) * n_lanes] = out_f32[half].astype(BF16).reshape(
-            n_src, 2 * n_chans, n_lanes)
-
-
-def channel_convs(sig, taps, skip):
-    n_src, n_both, n_tok = sig.shape
-    n_chans, n_lanes = n_both // 2, n_tok // 2
-    n_rows = 2 * n_src
-    tables = transform_tables(n_rows, n_lanes)
+                gfilt_ref[pl.ds(odd * n_chans + chan, n_dev, stride=2 * n_chans), :] = lin[
+                    odd * n_dev:(odd + 1) * n_dev, cols]
+
+    pairs(taps_grad)
+    wait_all(recv_sem, 2, y_ref)
+    wait_all(recv_sem, 3, du_ref)
+    for which, ref in enumerate((u_ref, dy_ref, y_out, du_out)):
+        wait_all(send_sem, which, ref)
+
+
+def mix_channels(u_cm, dy_cm, filt_taps, skip_gain):
+    n_dev, n_chans, n_tok = u_cm.shape
+    n_lanes = n_tok // 2
+    n_rows = 2 * n_dev
+    n_wide = 8
+    tables = [jnp.asarray(tab) for tab in transform_tables(n_rows, n_lanes)]
     vmem = pl.BlockSpec(memory_space=pltpu.VMEM)
+    hbm = pl.BlockSpec(memory_space=pl.ANY)
+    block = pltpu.VMEM(u_cm.shape, BF16)
+    flat = pltpu.VMEM((2, n_dev * n_chans, n_lanes), F32)
+    spec = pltpu.VMEM((n_chans // 2, 2 * n_rows, 2 * n_lanes), F32)
     return pl.pallas_call(
-        functools.partial(conv_kernel, n_chans),
+        mix_kernel,
         out_shape=(
-            jax.ShapeDtypeStruct(sig.shape, BF16),
+            jax.ShapeDtypeStruct(u_cm.shape, BF16),
+            jax.ShapeDtypeStruct(u_cm.shape, BF16),
             jax.ShapeDtypeStruct((n_rows * n_chans, n_lanes), F32),
             jax.ShapeDtypeStruct((n_chans, n_lanes), F32),
         ),
-        in_specs=[vmem, vmem, pl.BlockSpec(memory_space=pltpu.SMEM)] + [vmem] * 5,
-        out_specs=(vmem, vmem, vmem),
-        scratch_shapes=[
-            pltpu.VMEM((2, n_src * n_both, n_lanes), F32),
-            pltpu.VMEM((2, n_src * n_both, n_lanes), F32),
+        in_specs=[vmem, vmem, hbm, pl.BlockSpec(memory_space=pltpu.SMEM)] + [hbm] * 5,
+        out_specs=(vmem,) * 4,
+        scratch_shapes=[block] * 4 + [flat] * 3 + [
+            pltpu.VMEM((n_wide, n_rows * n_lanes // n_wide, 128), F32),
+            pltpu.VMEM((4, 128, n_lanes), F32),
+            pltpu.VMEM((n_rows * n_chans, n_lanes), F32),
+        ] + [spec] * 3 + [pltpu.VMEM(tab.shape, tab.dtype) for tab in tables] + [
+            pltpu.SemaphoreType.DMA((len(tables),)),
+            pltpu.SemaphoreType.DMA((n_wide,)),
+            pltpu.SemaphoreType.DMA((4,)),
+            pltpu.SemaphoreType.DMA((4,)),
         ],
-        compiler_params=pltpu.CompilerParams(vmem_limit_bytes=48 * 2 ** 20),
-        cost_estimate=pl.CostEstimate(flops=10 ** 10, bytes_accessed=8 * 2 ** 20, transcendentals=0),
-        name="channel_convs",
-    )(sig, taps, skip, *[jnp.asarray(tab) for tab in tables])
+        compiler_params=pltpu.CompilerParams(vmem_limit_bytes=60 * 2 ** 20, collective_id=1, has_side_effects=True),
+        cost_estimate=pl.CostEstimate(flops=10 ** 10, bytes_accessed=24 * 2 ** 20, transcendentals=0),
+        name="mix_channels",
+    )(u_cm, dy_cm, filt_taps, skip_gain, *tables)
 
 
 RING = 4
@@ -387,7 +512,6 @@
         n_chans = width // ctx_size
         seq_len = n_tok * ctx_size
         n_lanes = n_tok // 2
-        rank = lax.axis_index("cp")
         x_tok, do_tok = x_seq[0], d_out[0]
 
         def mm(a, b, ca, cb):
@@ -398,19 +522,11 @@
         u_act = k_act * v_act
         dz_act = mm(w_out, do_tok, 1, 1).astype(BF16)
         dy_act = dz_act * q_act
-        sig = jnp.concatenate([u_act.reshape(ctx_size, n_chans, n_tok), dy_act.reshape(ctx_size, n_chans, n_tok)], axis=1)
-        sig = lax.all_to_all(sig, "cp", 0, 0, tiled=True)
-
-        taps = lax.dynamic_slice_in_dim(filt_taps, rank * n_chans, n_chans, axis=1)
-        taps = taps.reshape(seq_len // n_lanes, n_lanes, n_chans).transpose(0, 2, 1).reshape(-1, n_lanes)
-        skip = lax.dynamic_slice_in_dim(skip_gain, rank * n_chans, n_chans, axis=0)
-        res, gfilt, gskip = channel_convs(sig, taps, skip)
+        by_dev = (ctx_size, n_chans, n_tok)
+        y_dev, du_dev, gfilt, gskip = mix_channels(u_act.reshape(by_dev), dy_act.reshape(by_dev), filt_taps, skip_gain)
         grad_filt = gfilt.reshape(seq_len // n_lanes, n_chans, n_lanes).transpose(0, 2, 1).reshape(seq_len, n_chans)
         grad_skip = jnp.sum(gskip, axis=1)
-
-        res = lax.all_to_all(res, "cp", 0, 0, tiled=True)
-        y_act = res[:, :n_chans].reshape(width, n_tok)
-        du_act = res[:, n_chans:].reshape(width, n_tok)
+        y_act, du_act = y_dev.reshape(width, n_tok), du_dev.reshape(width, n_tok)
         z_act = q_act * y_act
         d_qkv = jnp.concatenate([dz_act * y_act, du_act * v_act, du_act * k_act], axis=0)
         grad_x = mm(d_qkv, w_in, 0, 1).astype(BF16)[None]

time: 158 us -> 130 us (0.82)
  Pallas kernels: 67.9 us -> 107 us
  local copies, waits for them, and re-layouts: 33.7 us -> 4.03 us
  starting transfers between devices: 21.6 us -> 0 us
  waiting for transfers between devices: 16.1 us -> 0 us
    pallas_call x1, Pallas kernels: 17.9 us -> 53.9 us  [mix_channels(): pl.pallas_call(mix_kernel, out_shape=(jax.ShapeDtypeStruct(u_cm.shape, BF...]
    all_to_all x2 -> x0, starting transfers between devices: 21.6 us -> none  [the longest x1 11.7 us: local_step(): sig = lax.all_to_all(sig, 'cp', 0, 0, tiled=True)]
    all_to_all x2 -> x0, waiting for transfers between devices: 16.1 us -> none  [the longest x1 16.1 us: local_step(): res = lax.all_to_all(res, 'cp', 0, 0, tiled=True)]
    unnamed x23 -> x29, local copies, waits for them, and re-layouts: 18.1 us -> 3.04 us
    dynamic_slice x2 -> x0, local copies, waits for them, and re-layouts: 13.6 us -> none  [the longest x1 12.8 us: local_step(): taps = lax.dynamic_slice_in_dim(filt_taps, rank * n_chans, n_chans, axis=1)]
    pallas_call x1, Pallas kernels: 50 us -> 52.9 us  [weight_grads(): pl.pallas_call(functools.partial(grad_kernel, n_in), out_shape=(jax.Shape...]
    reshape x1, other arithmetic: 0.15 us -> 2.11 us  [local_step(): dy_act.reshape(by_dev)]
  transfers between devices with their start and end apart: 2 -> 0, of which waited for: 1 -> 0; matrix products, arithmetic and copies ran while one was open for 17% -> 0% of each run, Pallas kernels for 0% -> 0%
where the time goes in v2:
time: 130 us
  Pallas kernels  107 us (82%)
  matrix products  12 us (9%)
  other arithmetic  6.33 us (5%)
  local copies, waits for them, and re-layouts  4.03 us (3%)
    pallas_call x1, Pallas kernels, mix_channels(): pl.pallas_call(mix_kernel, out_shape=(jax.ShapeDtypeStruct(u_cm.shape, BF...  53.9 us
    pallas_call x1, Pallas kernels, weight_grads(): pl.pallas_call(functools.partial(grad_kernel, n_in), out_shape=(jax.Shape...  52.9 us
    dot_general x3, matrix products, mm(): lax.dot_general(a, b, (((ca,), (cb,)), ((), ())), preferred_element_type=...  12 us
    unnamed x29, local copies, waits for them, and re-layouts  3.04 us

profile of v2, /device:TPU:0, one launch (start us, length us, event | category | flops | bytes accessed | tf_op | source)
XLA Modules:
  0.0 129.8 jit_solution(14432828631467975740)
XLA Ops:
  0.6 0.0 copy-start
  0.6 0.0 copy-start.12
  0.7 4.9 %convolution_convert_fusion = bf16[3072,256]{1,0:T(8,128)(2,1)S(1)} fusion(bf16[1024,3072]{1,0:T(8,128)(2,1)} %param.12, bf16[1,256,1024]{2,1,0:T(8,128)(2,1)} %param.11), kind=kOutput, calls=%fused_computation | convolution fusion | flops 1611399168 | bytes 8388608 | tf_op jit(solution)/shard_map/dot_general | solution.py:518
  5.6 0.0 copy-done
  5.6 0.0 copy-done.12
  5.6 1.5 %convolution_convert_fusion.2 = bf16[1024,256]{1,0:T(8,128)(2,1)} fusion(bf16[1024,1024]{1,0:T(8,128)(2,1)S(1)} %copy-done, bf16[1,256,1024]{2,1,0:T(8,128)(2,1)S(1)} %copy-done.12), kind=kOutput, calls=%fused_computation.3 | convolution fusion | flops 537133056 | bytes 3145728 | tf_op jit(solution)/shard_map/dot_general | solution.py:518
  7.1 2.1 %multiply_bitcast_fusion = (bf16[128,8,256]{2,1,0:T(8,128)(2,1)}, bf16[128,8,256]{2,1,0:T(8,128)(2,1)}) fusion(bf16[1024,256]{1,0:T(8,128)(2,1)} %convolution_convert_fusion.2, bf16[3072,256]{1,0:T(8,128)(2,1)S(1)} %convolution_convert_fusion), kind=kLoop, calls=%fused_computation.10 | loop fusion | flops 524288 | bytes 3145728 | tf_op jit(solution)/shard_map/reshape | solution.py:526
  9.2 53.9 %mix_channels.1 = (bf16[128,8,256]{2,1,0:T(8,128)(2,1)}, bf16[128,8,256]{2,1,0:T(8,128)(2,1)}, f32[2048,128]{1,0:T(8,128)}, f32[8,128]{1,0:T(8,128)}) custom-call(bf16[128,8,256]{2,1,0:T(8,128)(2,1)} %get-tuple-element.21.u_ref, bf16[128,8,256]{2,1,0:T(8,128)(2,1)} %get-tuple-element.20.dy_ref, f32[32768,1024]{1,0:T(8,128)} %filt_ref.1, f32[1024]{0:T(1024)} %skip_ref.1, ...), custom_call_target="tpu_custom_call" | custom-call | flops 10000000000 | bytes 25165824 | tf_op jit(solution)/shard_map/mix_channels/pallas_call | solution.py:259
  63.1 2.3 %bitcast_multiply_fusion.1 = (bf16[1024,256]{1,0:T(8,128)(2,1)S(1)}, bf16[1024,256]{1,0:T(8,128)(2,1)S(1)}, bf16[1024,256]{1,0:T(8,128)(2,1)}, bf16[1024,256]{1,0:T(8,128)(2,1)S(1)}) fusion(bf16[128,8,256]{2,1,0:T(8,128)(2,1)} %get-tuple-element.12, bf16[3072,256]{1,0:T(8,128)(2,1)S(1)} %convolution_convert_fusion, ...), kind=kLoop, calls=%fused_computation.6 | loop fusion | flops 1048576 | bytes 5242880 | tf_op jit(solution)/shard_map/mul | solution.py:531
  65.5 0.8 copy-done.1
  66.2 1.3 pad_maximum_fusion.d_ref
  67.5 0.0 copy-done.3
  67.5 0.0 copy-done.5
  67.5 0.0 copy-done.8
  67.5 1.0 copy.16
  68.5 52.9 %weight_grads.1 = (bf16[8,3072]{1,0:T(8,128)(2,1)}, bf16[8,1024]{1,0:T(8,128)(2,1)}) custom-call(bf16[64,2,8,256]{3,2,1,0:T(8,128)(2,1)} %bitcast.33, bf16[64,2,8,256]{3,2,1,0:T(8,128)(2,1)} %bitcast.31, bf16[3072,256]{1,0:T(8,128)(2,1)} %pad_maximum_fusion.d_ref, bf16[256,1024]{1,0:T(8,128)(2,1)} %bitcast.34), custom_call_target="tpu_custom_call" | custom-call | flops 5000000000 | bytes 8388608 | tf_op jit(solution)/shard_map/weight_grads/pallas_call | solution.py:495
  121.4 0.0 copy-done.2
  121.4 0.0 copy-done.4
  121.4 0.0 copy-done.6
  121.4 0.0 copy-start.11
  121.5 0.0 copy-start.9
  121.5 0.0 copy-start.10
  121.5 0.0 copy-start.7
  121.5 5.5 %fusion = bf16[1,256,1024]{2,1,0:T(8,128)(2,1)} fusion(bf16[1024,3072]{1,0:T(8,128)(2,1)} %param.12, bf16[1024,256]{1,0:T(8,128)(2,1)S(1)} %copy-done.4, bf16[1024,256]{1,0:T(8,128)(2,1)S(1)} %copy-done.2, bf16[1024,256]{1,0:T(8,128)(2,1)S(1)} %copy-done.6), kind=kOutput, calls=%fused_computation.4 | convolution fusion | flops 1615593472 | bytes 8388608 | tf_op jit(solution)/shard_map/dot_general | solution.py:518
  127.0 0.0 copy-done.11
  127.0 0.6 reduce_sum.9
  127.6 0.0 copy-done.9
  127.6 0.6 copy.20
  128.2 0.0 copy-done.10
  128.2 0.6 copy.21
  128.9 0.0 copy-done.7
  128.9 1.0 copy.22
  (7 shorter events, 0.0 us)
Async XLA Ops:
  0.6 4.9 %copy-start = (bf16[1024,1024]{1,0:T(8,128)(2,1)S(1)}, bf16[1024,1024]{1,0:T(8,128)(2,1)}, u32[]{:S(2)}) copy-start(bf16[1024,1024]{1,0:T(8,128)(2,1)} %param.13) | copy-start | bytes 6291460
  0.6 4.9 %copy-start.12 = (bf16[1,256,1024]{2,1,0:T(8,128)(2,1)S(1)}, bf16[1,256,1024]{2,1,0:T(8,128)(2,1)}, u32[]{:S(2)}) copy-start(bf16[1,256,1024]{2,1,0:T(8,128)(2,1)} %param.16) | copy-start | bytes 1572868
  65.4 0.8 copy-start.1
  65.5 2.1 %copy-start.3 = (bf16[1024,256]{1,0:T(8,128)(2,1)}, bf16[1024,256]{1,0:T(8,128)(2,1)S(1)}, u32[]{:S(2)}) copy-start(bf16[1024,256]{1,0:T(8,128)(2,1)S(1)} %get-tuple-element.18) | copy-start | bytes 1572868
  65.5 2.1 %copy-start.5 = (bf16[1024,256]{1,0:T(8,128)(2,1)}, bf16[1024,256]{1,0:T(8,128)(2,1)S(1)}, u32[]{:S(2)}) copy-start(bf16[1024,256]{1,0:T(8,128)(2,1)S(1)} %get-tuple-element.22) | copy-start | bytes 1572868
  65.5 2.1 %copy-start.8 = (bf16[1,256,1024]{2,1,0:T(8,128)(2,1)S(1)}, bf16[1,256,1024]{2,1,0:T(8,128)(2,1)}, u32[]{:S(2)}) copy-start(bf16[1,256,1024]{2,1,0:T(8,128)(2,1)} %param.11) | copy-start | bytes 1572868
  68.5 52.9 %copy-start.2 = (bf16[1024,256]{1,0:T(8,128)(2,1)S(1)}, bf16[1024,256]{1,0:T(8,128)(2,1)}, u32[]{:S(2)}) copy-start(bf16[1024,256]{1,0:T(8,128)(2,1)} %copy-done.1) | copy-start | bytes 1572868
  68.5 52.9 %copy-start.4 = (bf16[1024,256]{1,0:T(8,128)(2,1)S(1)}, bf16[1024,256]{1,0:T(8,128)(2,1)}, u32[]{:S(2)}) copy-start(bf16[1024,256]{1,0:T(8,128)(2,1)} %copy-done.3) | copy-start | bytes 1572868
  68.5 52.9 %copy-start.6 = (bf16[1024,256]{1,0:T(8,128)(2,1)S(1)}, bf16[1024,256]{1,0:T(8,128)(2,1)}, u32[]{:S(2)}) copy-start(bf16[1024,256]{1,0:T(8,128)(2,1)} %copy-done.5) | copy-start | bytes 1572868
  121.4 5.6 %copy-start.11 = (f32[8,128]{1,0:T(8,128)S(1)}, f32[8,128]{1,0:T(8,128)}, u32[]{:S(2)}) copy-start(f32[8,128]{1,0:T(8,128)} %get-tuple-element.16) | copy-start | bytes 12292
  121.5 6.2 %copy-start.9 = (bf16[8,3072]{1,0:T(8,128)(2,1)S(1)}, bf16[8,3072]{1,0:T(8,128)(2,1)}, u32[]{:S(2)}) copy-start(bf16[8,3072]{1,0:T(8,128)(2,1)} %get-tuple-element.29) | copy-start | bytes 147460
  121.5 6.8 %copy-start.10 = (bf16[8,1024]{1,0:T(8,128)(2,1)S(1)}, bf16[8,1024]{1,0:T(8,128)(2,1)}, u32[]{:S(2)}) copy-start(bf16[8,1024]{1,0:T(8,128)(2,1)} %get-tuple-element.30) | copy-start | bytes 49156
  121.5 7.4 %copy-start.7 = (f32[2048,128]{1,0:T(8,128)S(1)}, f32[2048,128]{1,0:T(8,128)}, u32[]{:S(2)}) copy-start(f32[2048,128]{1,0:T(8,128)} %get-tuple-element.15) | copy-start | bytes 3145732

commit v3 on v2

v3 whole, which is shorter than its diff:
```python
import functools

import jax
import jax.numpy as jnp
import numpy as np
from jax import lax
from jax.experimental import pallas as pl
from jax.experimental.pallas import tpu as pltpu
from jax.sharding import PartitionSpec as P

F32, BF16 = jnp.float32, jnp.bfloat16


def split_const(mat):
    hi = mat.astype(np.float32).astype(jnp.bfloat16)
    lo = (mat - hi.astype(np.float64)).astype(np.float32).astype(jnp.bfloat16)
    return hi, lo


@functools.lru_cache(None)
def transform_tables(n_rows, n_lanes):
    n = n_rows * n_lanes
    t1 = np.concatenate([np.arange(0, n_rows, 2), np.arange(1, n_rows, 2)])
    k1 = np.arange(n_rows)
    ang = 2 * np.pi * np.outer(k1 + 0.25, t1) / n_rows
    f1 = np.concatenate([np.cos(ang), -np.sin(ang)], axis=0)
    g1 = f1.T / n
    t2 = np.arange(n_lanes)
    psi = 2 * np.pi * (np.outer(t2, t2) % n_lanes) / n_lanes
    cos2, sin2 = np.cos(psi), np.sin(psi)
    f2 = np.block([[cos2, -sin2], [sin2, cos2]])
    g2 = f2.T
    twist = 2 * np.pi * np.outer(k1 + 0.25, t2) / n
    twid = np.concatenate([np.cos(twist), -np.sin(twist)], axis=1).astype(np.float32)
    f1h, f1l = split_const(f1)
    g1h, g1l = split_const(g1)
    f2h, f2l = split_const(f2)
    g2h, g2l = split_const(g2)
    return (
        np.concatenate([f1h, f1l], axis=1),
        np.concatenate([f2h, f2l], axis=0),
        np.concatenate([g2h, g2l], axis=0),
        np.concatenate([g1h, g1l], axis=1),
        twid,
    )


def dot(a, b):
    return jnp.dot(a, b, preferred_element_type=F32)


def halves(val):
    hi = val.astype(BF16)
    lo = (val - hi.astype(F32)).astype(BF16)
    return hi, lo


RING = 4
PART_ORDERS = ((0, 1, 2), (1, 2, 0), (2, 0, 1))


def part_columns(total):
    tiles = total // 128
    ends = [0, (tiles + 2) // 3 * 128, ((tiles + 2) // 3 + (tiles + 1) // 3) * 128, total]
    return [(ends[i], ends[i + 1]) for i in range(3)]


def hyena_kernel(qkv_ref, dz_ref, x_ref, do_ref, filt_ref, skip_ref, win_hbm, f1_hbm, f2_hbm, g2_hbm, g1_hbm, tw_hbm,
                 gx_ref, gwin_ref, gwout_ref, gfilt_ref, gskip_ref, *scratch):
    names = iter(scratch)

    def take(count):
        return [next(names) for _ in range(count)]

    u_out, dy_out, y_out, du_out, u_in, dy_in, y_in, du_in = take(8)
    u_f32, dy_f32, out_f32 = take(3)
    wide, flip, taps = take(3)
    u_spec, h_spec, d_spec = take(3)
    f1_ref, f2_ref, g2_ref, g1_ref, tw_ref, win_ref = take(6)
    z_own, d_own, x_peer, z_peer, d_peer, do_peer = take(6)
    partial = take(6)
    vias, fins, reds = [], [], []
    for phase in range(3):
        vias.append(take(6))
        fins.append(take(6))
        if phase < 2:
            reds.append(take(6))
    load_sem, wide_sem, ex_send, ex_recv, swap_send, swap_recv, ring_send, ring_recv = take(8)

    n_dev, n_chans, n_tok = u_out.shape
    n_lanes = n_tok // 2
    n_rows = 2 * n_dev
    n_pairs = n_chans // 2
    width = n_dev * n_chans
    rank = lax.axis_index("cp")
    core = lax.rem(rank, 2)
    chip = lax.div(rank, 2)
    coords = (lax.div(chip, 16), lax.rem(lax.div(chip, 4), 4), lax.rem(chip, 4))
    strides = (32, 8, 2)
    peer = rank + 1 - 2 * core

    def remote(src, dst, send, recv, device):
        return pltpu.make_async_remote_copy(src_ref=src, dst_ref=dst, send_sem=send, recv_sem=recv,
                                            device_id={"cp": device}, device_id_type=pl.DeviceIdType.MESH)

    def others(body):
        def step(i, carry):
            body(lax.rem(rank + i, n_dev))
            return carry

        lax.fori_loop(1, n_dev, step, 0)

    barrier = pltpu.get_barrier_semaphore()
    others(lambda dev: pl.semaphore_signal(barrier, inc=1, device_id={"cp": dev}, device_id_type=pl.DeviceIdType.MESH))

    n_slot, per_slot = wide.shape[0], wide.shape[1]
    n_wide = filt_ref.shape[0] // per_slot
    first_lane = pl.multiple_of(lax.div(rank * n_chans, 128) * 128, 128)
    wides = [pltpu.make_async_copy(
        filt_ref.at[pl.ds(i * per_slot, per_slot), pl.ds(first_lane, 128)], wide.at[i % n_slot], wide_sem.at[i])
        for i in range(n_wide)]
    loads = [pltpu.make_async_copy(src, dst, load_sem.at[i]) for i, (src, dst) in enumerate(
        ((f1_hbm, f1_ref), (f2_hbm, f2_ref), (g2_hbm, g2_ref), (g1_hbm, g1_ref), (tw_hbm, tw_ref), (win_hbm, win_ref)))]
    for copy in wides[:n_slot] + loads:
        copy.start()

    def act(i):
        return qkv_ref[i * width:(i + 1) * width]

    u_out[...] = (act(1) * act(2)).reshape(u_out.shape)
    dy_out[...] = (dz_ref[...] * act(0)).reshape(dy_out.shape)
    pl.semaphore_wait(barrier, n_dev - 1)

    def exchange(which, src, dst):
        others(lambda dev: remote(src.at[dev], dst.at[rank], ex_send.at[which], ex_recv.at[which], dev).start())
        dst[rank] = src[rank]

    def wait_all(sem, which, ref):
        part = ref.at[pl.ds(0, n_dev - 1)]
        pltpu.make_async_copy(part, part, sem.at[which]).wait()

    exchange(0, u_out, u_in)
    exchange(1, dy_out, dy_in)

    swaps = []

    def swap(src, dst):
        copy = remote(src, dst, swap_send.at[len(swaps)], swap_recv.at[len(swaps)], peer)
        copy.start()
        swaps.append(copy)
        return copy

    x_swap = swap(x_ref.at[:, 1 - core], x_peer)
    do_swap = swap(do_ref, do_peer)

    own_row = pl.multiple_of(lax.rem(rank * n_chans, 128), n_chans)
    per_wide = per_slot // n_lanes

    for i in range(n_wide):
        wides[i].wait()

        def turn(j, carry):
            for k in range(4):
                tile = 4 * j + k
                flip[k] = wide[i % n_slot, pl.ds(pl.multiple_of(tile * n_lanes, n_lanes), n_lanes), :].T
                at = pl.multiple_of((i * per_wide + tile) * n_chans, n_chans)
                taps[pl.ds(at, n_chans), :] = flip[k, pl.ds(own_row, n_chans), :]
            return carry

        lax.fori_loop(0, per_wide // 4, turn, 0)
        if i + n_slot < n_wide:
            wides[i + n_slot].start()
    for copy in loads[:5]:
        copy.wait()

    def f1(i):
        return f1_ref[:, i * n_rows:(i + 1) * n_rows]

    def g1(i):
        return g1_ref[:, 2 * i * n_rows:2 * (i + 1) * n_rows]

    def f2(i):
        return f2_ref[2 * i * n_lanes:2 * (i + 1) * n_lanes]

    def g2(i):
        return g2_ref[2 * i * n_lanes:2 * (i + 1) * n_lanes]

    def twist():
        return tw_ref[:, :n_lanes], tw_ref[:, n_lanes:]

    def second(stage):
        wr, wi = twist()
        parts = []
        for i in range(2):
            ar = stage[:n_rows, i * n_lanes:(i + 1) * n_lanes]
            ai = stage[n_rows:, i * n_lanes:(i + 1) * n_lanes]
            parts.append(jnp.concatenate([ar * wr - ai * wi, ar * wi + ai * wr], axis=1))
        bh, bl = halves(jnp.concatenate(parts, axis=0))
        return dot(bh, f2(0)) + (dot(bh, f2(1)) + dot(bl, f2(0)))

    def inverse(pr, pi):
        wr, wi = twist()
        ph, pll = halves(jnp.concatenate([pr, pi], axis=1))
        mid = dot(ph, g2(0)) + (dot(ph, g2(1)) + dot(pll, g2(0)))
        tr, ti = [], []
        for i in range(2):
            gr = mid[i * n_rows:(i + 1) * n_rows, :n_lanes]
            gi = mid[i * n_rows:(i + 1) * n_rows, n_lanes:]
            tr.append(gr * wr + gi * wi)
            ti.append(gi * wr - gr * wi)
        th, tl = halves(jnp.concatenate([jnp.concatenate(tr, axis=1), jnp.concatenate(ti, axis=1)], axis=0))
        return dot(g1(0), th) + (dot(g1(0), tl) + dot(g1(1), th))

    def pairs(body):
        def step(p, carry):
            body(p)
            return carry

        lax.fori_loop(0, n_pairs, step, 0)

    def rows_of(ref, chan):
        return jnp.concatenate([ref[0, pl.ds(chan, n_dev, stride=n_chans), :],
                                ref[1, pl.ds(chan, n_dev, stride=n_chans), :]], axis=0)

    def both(ref, p):
        return jnp.concatenate([rows_of(ref, 2 * p), rows_of(ref, 2 * p + 1)], axis=1)

    def widen(src, dst):
        for half in range(2):
            dst[half] = src[:, :, half * n_lanes:(half + 1) * n_lanes].astype(F32).reshape(dst.shape[1:])

    def parts_of(ref, p):
        return ref[p, :, :n_lanes], ref[p, :, n_lanes:]

    def taps_spec(p):
        def one(chan):
            return jnp.concatenate([taps[pl.ds(chan, n_dev, stride=2 * n_chans), :],
                                    taps[pl.ds(n_chans + chan, n_dev, stride=2 * n_chans), :]], axis=0)

        h_hi, h_lo = halves(jnp.concatenate([one(2 * p), one(2 * p + 1)], axis=1))
        h_spec[p] = second(dot(f1(0), h_hi) + (dot(f1(0), h_lo) + dot(f1(1), h_hi)))

    pairs(taps_spec)

    def filtered(sig, spec, sign):
        def one(p):
            val = both(sig, p)
            low = val.astype(BF16)
            spec[p] = second(dot(f1(0), low) + dot(f1(1), low))
            sr, si = parts_of(spec, p)
            hr, hi = parts_of(h_spec, p)
            if sign > 0:
                lin = inverse(sr * hr - si * hi, sr * hi + si * hr)
            else:
                lin = inverse(sr * hr + si * hi, si * hr - sr * hi)
            for i in range(2):
                chan = 2 * p + i
                cols = slice(i * n_lanes, (i + 1) * n_lanes)
                res = lin[:, cols] + skip_ref[rank * n_chans + chan] * val[:, cols]
                for odd in range(2):
                    out_f32[odd, pl.ds(chan, n_dev, stride=n_chans), :] = res[odd * n_dev:(odd + 1) * n_dev]

        pairs(one)

    def narrow(dst):
        for half in range(2):
            dst[:, :, half * n_lanes:(half + 1) * n_lanes] = out_f32[half].astype(BF16).reshape(
                n_dev, n_chans, n_lanes)

    wait_all(ex_recv, 0, u_in)
    widen(u_in, u_f32)
    filtered(u_f32, u_spec, 1)
    narrow(y_out)
    exchange(2, y_out, y_in)
    wait_all(ex_recv, 1, dy_in)
    widen(dy_in, dy_f32)
    filtered(dy_f32, d_spec, -1)
    narrow(du_out)
    exchange(3, du_out, du_in)

    wait_all(ex_recv, 2, y_in)
    y_act = y_in[...].reshape(width, n_tok)
    z_own[...] = (act(0) * y_act).reshape(z_own.shape)
    d_own[0:width] = dz_ref[...] * y_act
    z_swap = swap(z_own.at[:, 1 - core], z_peer)
    d_swaps = [swap(d_own.at[pl.ds(0, width)], d_peer.at[pl.ds(0, width)])]

    def taps_grad(p):
        ur, ui = parts_of(u_spec, p)
        dr, di = parts_of(d_spec, p)
        lin = inverse(dr * ur + di * ui, di * ur - dr * ui)
        prod = both(u_f32, p) * both(dy_f32, p)
        for i in range(2):
            chan = 2 * p + i
            cols = slice(i * n_lanes, (i + 1) * n_lanes)
            gskip_ref[pl.ds(chan, 1), :] = jnp.sum(prod[:, cols], axis=0, keepdims=True)
            for odd in range(2):
                gfilt_ref[pl.ds(odd * n_chans + chan, n_dev, stride=2 * n_chans), :] = lin[
                    odd * n_dev:(odd + 1) * n_dev, cols]

    pairs(taps_grad)

    def at_offset(dim, step):
        pos = lax.rem(coords[dim] + step, RING)
        return pos, rank + (pos - coords[dim]) * strides[dim]

    nxt = [at_offset(dim, 1) for dim in range(3)]
    opp = [at_offset(dim, 2) for dim in range(3)]
    prv = [at_offset(dim, 3) for dim in range(3)]
    cols = part_columns(2 * width)
    half_rows = width // 2

    def mm(a, b, cb):
        return lax.dot_general(a, b, (((1,), (cb,)), ((), ())), preferred_element_type=F32)

    def flat(val):
        return val.reshape(half_rows, n_tok)

    def segments(part):
        lo, hi = cols[part % 3]
        runs = []
        for first, is_out, base in (((0, False, 0), (width, True, 0)) if part < 3 else ((0, False, width),)):
            last = first + width if part < 3 else 2 * width
            a, b = max(lo, first), min(hi, last)
            if a < b:
                runs.append((is_out, base + a - first, a - lo, b - a))
        return runs

    def products(part):
        for is_out, first, place, size in segments(part):
            for off in range(0, size, 512):
                step = min(512, size - off)
                at = first + off
                if is_out:
                    val = (mm(flat(z_own[:, core]), do_ref[:, at:at + step], 0)
                           + mm(flat(z_peer[...]), do_peer[:, at:at + step], 0))
                else:
                    val = (mm(flat(x_ref[:, core]), d_own[at:at + step], 1)
                           + mm(flat(x_peer[...]), d_peer[at:at + step], 1))
                partial[part][:, :, :, :, place + off:place + off + step] = val.reshape(
                    RING, RING, RING, n_chans, step)

    def slab(ref, axis, pos, col=None):
        index = [slice(None)] * len(ref.shape)
        if axis is not None:
            index[axis] = pos
        if col is not None:
            index[-1] = pl.ds(*col)
        return ref.at[tuple(index)]

    copies = {}

    def send(part, phase, which, src, dst, device):
        slot = (phase * 6 + part) * 6 + which
        copy = remote(src, dst, ring_send.at[slot], ring_recv.at[slot], device)
        copy.start()
        copies[part, phase, which] = copy

    def setting(part, phase):
        order = PART_ORDERS[(part + part // 3) % 3]
        dim = order[phase]
        axis = sorted(order[phase:]).index(dim)
        src = partial[part] if phase == 0 else reds[phase - 1][part]
        size = src.shape[-1]
        first = (size // 128 + 1) // 2 * 128
        return dim, axis, src, vias[phase][part], fins[phase][part], (0, first), (first, size - first)

    def launch(part, phase):
        dim, axis, src, via, fin, a_cols, b_cols = setting(part, phase)
        send(part, phase, 0, slab(src, axis, opp[dim][0], a_cols), slab(via, None, None, a_cols), nxt[dim][1])
        send(part, phase, 1, slab(src, axis, opp[dim][0], b_cols), slab(via, None, None, b_cols), prv[dim][1])
        send(part, phase, 2, slab(src, axis, nxt[dim][0], b_cols), slab(fin, 0, 0, b_cols), nxt[dim][1])
        send(part, phase, 3, slab(src, axis, prv[dim][0], a_cols), slab(fin, 0, 1, a_cols), prv[dim][1])

    def each_block(shape, body):
        lead = shape[:-2]
        count = int(np.prod(lead)) if lead else 1
        if count == 1:
            body(tuple(0 for _ in lead))
            return

        def step(i, carry):
            index = []
            for size in reversed(lead):
                index.insert(0, lax.rem(i, size))
                i = lax.div(i, size)
            body(tuple(index))
            return carry

        lax.fori_loop(0, count, step, 0, unroll=min(count, 4))

    def relay(part, phase):
        dim, axis, src, via, fin, a_cols, b_cols = setting(part, phase)
        for which, col, spot, side in ((0, a_cols, nxt[dim], 0), (1, b_cols, prv[dim], 1)):
            copies[part, phase, which].wait_recv()
            span = pl.ds(*col)

            def add(index):
                at = index[:axis] + (spot[0],) + index[axis:]
                src[at + (slice(None), span)] = src[at + (slice(None), span)] + via[index + (slice(None), span)]

            each_block(via.shape, add)
            send(part, phase, 4 + which, slab(src, axis, spot[0], col), slab(fin, 0, side, col), spot[1])

    def finish(part, phase):
        dim, axis, src, via, fin, _, _ = setting(part, phase)
        for which in range(2, 6):
            copies[part, phase, which].wait_recv()

        def add(index):
            at = index[:axis] + (coords[dim],) + index[axis:]
            total = src[at] + fin[(0,) + index] + fin[(1,) + index]
            if phase < 2:
                reds[phase][part][index] = total
                return
            for is_out, first, place, size in segments(part):
                dst = gwout_ref if is_out else gwin_ref
                dst[:, first:first + size] = total[:, place:place + size].astype(dst.dtype)

        each_block(via.shape, add)
        if phase < 2:
            launch(part, phase + 1)

    early, late = (0, 1, 2), (3, 4, 5)
    for copy in (x_swap, do_swap, z_swap, d_swaps[0]):
        copy.wait_recv()
    for part in early:
        products(part)
        launch(part, 0)

    wait_all(ex_recv, 3, du_in)
    du_act = du_in[...].reshape(width, n_tok)
    for i in (1, 2):
        d_own[i * width:(i + 1) * width] = du_act * act(3 - i)
        span = pl.ds(i * width, width)
        d_swaps.append(swap(d_own.at[span], d_peer.at[span]))

    def run(step, parts, phase):
        for part in parts:
            step(part, phase)

    run(relay, early, 0)
    for copy in d_swaps[1:]:
        copy.wait_recv()
    for part in late:
        products(part)
        launch(part, 0)

    loads[5].wait()
    for first in range(0, width, 256):
        gx_ref[:, first:first + 256] = dot(win_ref[first:first + 256], d_own[...]).T.astype(gx_ref.dtype)

    run(finish, early, 0)
    run(relay, late, 0)
    run(relay, early, 1)
    run(finish, early, 1)
    run(finish, late, 0)
    run(relay, early, 2)
    run(finish, early, 2)
    run(relay, late, 1)
    run(finish, late, 1)
    run(relay, late, 2)
    run(finish, late, 2)
    for which, ref in enumerate((u_out, dy_out, y_out, du_out)):
        wait_all(ex_send, which, ref)
    for copy in list(copies.values()) + swaps:
        copy.wait_send()


def hyena_grads(qkv, dz, x_cm, d_out, filt_taps, skip_gain, w_in, n_dev):
    n_chip, n_core, n_chans, n_tok = x_cm.shape
    width = dz.shape[0]
    n_lanes, n_rows = n_tok // 2, 2 * n_dev
    n_taps = filt_taps.shape[0]
    n_wide, n_slot = 8, 4
    tables = [jnp.asarray(tab) for tab in transform_tables(n_rows, n_lanes)]
    vmem = pl.BlockSpec(memory_space=pltpu.VMEM)
    hbm = pl.BlockSpec(memory_space=pl.ANY)
    widths = [hi - lo for lo, hi in part_columns(2 * width)] * 2
    scratch = [pltpu.VMEM((n_dev, n_chans, n_tok), BF16)] * 8
    scratch += [pltpu.VMEM((2, width, n_lanes), F32)] * 3
    scratch += [pltpu.VMEM((n_slot, n_taps // n_wide, 128), F32), pltpu.VMEM((4, 128, n_lanes), F32),
                pltpu.VMEM((n_rows * n_chans, n_lanes), F32)]
    scratch += [pltpu.VMEM((n_chans // 2, 2 * n_rows, 2 * n_lanes), F32)] * 3
    scratch += [pltpu.VMEM(arr.shape, arr.dtype) for arr in tables + [w_in]]
    scratch += [pltpu.VMEM(x_cm.shape, BF16), pltpu.VMEM(qkv.shape, BF16), pltpu.VMEM((n_chip, n_chans, n_tok), BF16),
                pltpu.VMEM((n_chip, n_chans, n_tok), BF16), pltpu.VMEM(qkv.shape, BF16), pltpu.VMEM(d_out.shape, BF16)]
    scratch += [pltpu.VMEM((RING,) * 3 + (n_chans, w), F32) for w in widths]
    for n_lead in (2, 1, 0):
        lead = (RING,) * n_lead
        scratch += [pltpu.VMEM(lead + (n_chans, w), F32) for w in widths]
        scratch += [pltpu.VMEM((2,) + lead + (n_chans, w), F32) for w in widths]
        if n_lead:
            scratch += [pltpu.VMEM(lead + (n_chans, w), F32) for w in widths]
    scratch += [pltpu.SemaphoreType.DMA((n,)) for n in (len(tables) + 1, n_wide, 4, 4, 6, 6, 108, 108)]
    return pl.pallas_call(
        hyena_kernel,
        out_shape=(
            jax.ShapeDtypeStruct((n_tok, width), BF16),
            jax.ShapeDtypeStruct((n_chans, 3 * width), BF16),
            jax.ShapeDtypeStruct((n_chans, width), BF16),
            jax.ShapeDtypeStruct((n_rows * n_chans, n_lanes), F32),
            jax.ShapeDtypeStruct((n_chans, n_lanes), F32),
        ),
        in_specs=[vmem] * 4 + [hbm, pl.BlockSpec(memory_space=pltpu.SMEM)] + [hbm] * 6,
        out_specs=(vmem,) * 5,
        scratch_shapes=scratch,
        compiler_params=pltpu.CompilerParams(vmem_limit_bytes=63 * 2 ** 20, collective_id=0, has_side_effects=True),
        cost_estimate=pl.CostEstimate(flops=2 * 10 ** 10, bytes_accessed=32 * 2 ** 20, transcendentals=0),
        name="hyena_grads",
    )(qkv, dz, x_cm, d_out, filt_taps, skip_gain, w_in, *tables)


def solution(mesh):
    ctx_size = mesh.shape["cp"]

    def local_step(x_seq, w_in, w_out, filt_taps, skip_gain, d_out):
        n_batch, n_tok, width = x_seq.shape
        n_chans = width // ctx_size
        seq_len = n_tok * ctx_size
        n_lanes = n_tok // 2
        x_tok, do_tok = x_seq[0], d_out[0]

        def mm(a, b, ca, cb):
            return lax.dot_general(a, b, (((ca,), (cb,)), ((), ())), preferred_element_type=F32)

        qkv = mm(w_in, x_tok, 0, 1).astype(BF16)
        dz = mm(w_out, do_tok, 1, 1).astype(BF16)
        x_cm = x_tok.T.reshape(ctx_size // 2, 2, n_chans, n_tok)
        grad_x, grad_w_in, grad_w_out, gfilt, gskip = hyena_grads(
            qkv, dz, x_cm, do_tok, filt_taps, skip_gain, w_in, ctx_size)
        grad_filt = gfilt.reshape(seq_len // n_lanes, n_chans, n_lanes).transpose(0, 2, 1).reshape(seq_len, n_chans)
        return grad_x[None], grad_w_in, grad_w_out, grad_filt, jnp.sum(gskip, axis=1)

    seq_spec = P("dp", "cp", None)
    row_spec = P(("dp", "cp"), None)
    return jax.shard_map(
        local_step,
        mesh=mesh,
        in_specs=(seq_spec, P(), P(), P(), P(), seq_spec),
        out_specs=(seq_spec, row_spec, row_spec, P("dp", "cp"), P(("dp", "cp"))),
        check_vma=False,
    )
```

time: 130 us -> 122 us (0.938)
  other arithmetic: 6.33 us -> 1.31 us
  Pallas kernels: 107 us -> 102 us
  local copies, waits for them, and re-layouts: 4.03 us -> 7.87 us
  matrix products: 12 us -> 9.11 us
    pallas_call x2 -> x1, Pallas kernels: 107 us -> 102 us  [hyena_grads(): pl.pallas_call(hyena_kernel, out_shape=(jax.ShapeDtypeStruct((n_tok, widt...]
    unnamed x29 -> x6, local copies, waits for them, and re-layouts: 3.04 us -> 6.88 us
    dot_general x3 -> x2, matrix products: 12 us -> 9.11 us  [mm(): lax.dot_general(a, b, (((ca,), (cb,)), ((), ())), preferred_element_type=...]
    mul x1 -> x0, other arithmetic: 2.33 us -> none  [local_step(): du_act * v_act]
    reshape x1 -> x0, other arithmetic: 2.11 us -> none  [local_step(): dy_act.reshape(by_dev)]
where the time goes in v3:
time: 122 us; the launch traced here: 121 us
  Pallas kernels  102 us (84%)
  matrix products  9.11 us (7%)
  local copies, waits for them, and re-layouts  7.87 us (6%)
  other arithmetic  1.31 us (1%)
    pallas_call x1, Pallas kernels, hyena_grads(): pl.pallas_call(hyena_kernel, out_shape=(jax.ShapeDtypeStruct((n_tok, widt...  102 us
    dot_general x2, matrix products, mm(): lax.dot_general(a, b, (((ca,), (cb,)), ((), ())), preferred_element_type=...  9.11 us
    unnamed x6, local copies, waits for them, and re-layouts  6.88 us

profile of v3, /device:TPU:0, one launch (start us, length us, event | category | flops | bytes accessed | tf_op | source)
XLA Modules:
  0.0 121.3 jit_solution(11690888376744967457)
XLA Ops:
  0.6 0.0 copy-start
  0.6 3.3 %convolution_convert_fusion.1.dz_ref = bf16[1024,256]{1,0:T(8,128)(2,1)} fusion(bf16[1024,1024]{1,0:T(8,128)(2,1)} %param.13, bf16[1,256,1024]{2,1,0:T(8,128)(2,1)} %param.16), kind=kOutput, calls=%fused_computation.1 | convolution fusion | flops 537133056 | bytes 3145728 | tf_op jit(solution)/shard_map/dot_general | solution.py:525
  3.9 0.0 copy-done
  3.9 1.0 copy.16
  4.9 5.8 %convolution_convert_fusion.qkv_ref = bf16[3072,256]{1,0:T(8,128)(2,1)} fusion(bf16[1024,3072]{1,0:T(8,128)(2,1)} %win_hbm.1, bf16[1,256,1024]{2,1,0:T(8,128)(2,1)S(1)} %copy-done), kind=kOutput, calls=%fused_computation | convolution fusion | flops 1611399168 | bytes 8388608 | tf_op jit(solution)/shard_map/dot_general | solution.py:525
  10.8 102.4 %hyena_grads.1 = (bf16[256,1024]{1,0:T(8,128)(2,1)}, bf16[8,3072]{1,0:T(8,128)(2,1)}, bf16[8,1024]{1,0:T(8,128)(2,1)}, f32[2048,128]{1,0:T(8,128)}, f32[8,128]{1,0:T(8,128)}) custom-call(bf16[3072,256]{1,0:T(8,128)(2,1)} %convolution_convert_fusion.qkv_ref, bf16[1024,256]{1,0:T(8,128)(2,1)} %convolution_convert_fusion.1.dz_ref, ...), custom_call_target="tpu_custom_call" | custom-call | flops 20000000000 | bytes 33554432 | tf_op jit(solution)/shard_map/hyena_grads/pallas_call | solution.py:496
  113.2 1.3 %reduce_sum.9 = f32[8]{0:T(128)} reduce(f32[8,128]{1,0:T(8,128)} %get-tuple-element.14, f32[]{:T(128)} %constant.5.clone.1), dimensions={1}, to_apply=%region_0.0 | reduce | flops 1016 | bytes 4132 | tf_op jit(solution)/shard_map/reduce_sum | solution.py:533
  114.5 1.9 %copy.21 = bf16[1,256,1024]{2,1,0:T(8,128)(2,1)} copy(bf16[1,256,1024]{2,1,0:T(8,128)(2,1)} %bitcast.21) | data formatting | bytes 1048576
  116.3 1.4 %copy.22 = bf16[8,3072]{1,0:T(8,128)(2,1)} copy(bf16[8,3072]{1,0:T(8,128)(2,1)} %get-tuple-element.21) | data formatting | bytes 98304
  117.8 1.3 %copy.23 = bf16[8,1024]{1,0:T(8,128)(2,1)} copy(bf16[8,1024]{1,0:T(8,128)(2,1)} %get-tuple-element.22) | data formatting | bytes 32768
  119.1 2.3 %copy.24 = f32[32768,8]{0,1:T(8,128)} copy(f32[32768,8]{0,1:T(8,128)} %bitcast.18) | data formatting | bytes 2097152
Async XLA Ops:
  0.6 3.3 %copy-start = (bf16[1,256,1024]{2,1,0:T(8,128)(2,1)S(1)}, bf16[1,256,1024]{2,1,0:T(8,128)(2,1)}, u32[]{:S(2)}) copy-start(bf16[1,256,1024]{2,1,0:T(8,128)(2,1)} %param.11) | copy-start | bytes 1572868

commit v4 on v3

--- a/solution.py
+++ b/solution.py
@@ -65,19 +65,21 @@
     return [(ends[i], ends[i + 1]) for i in range(3)]
 
 
-def hyena_kernel(qkv_ref, dz_ref, x_ref, do_ref, filt_ref, skip_ref, win_hbm, f1_hbm, f2_hbm, g2_hbm, g1_hbm, tw_hbm,
+def hyena_kernel(x_ref, do_ref, filt_ref, skip_ref, win_hbm, wout_hbm, f1_hbm, f2_hbm, g2_hbm, g1_hbm, tw_hbm,
                  gx_ref, gwin_ref, gwout_ref, gfilt_ref, gskip_ref, *scratch):
     names = iter(scratch)
 
     def take(count):
         return [next(names) for _ in range(count)]
 
-    u_out, dy_out, y_out, du_out, u_in, dy_in, y_in, du_in = take(8)
+    u_out, dy_out, u_in, dy_in, y_in, du_in = take(6)
+    y_out, du_out = u_in, dy_in
     u_f32, dy_f32, out_f32 = take(3)
     wide, flip, taps = take(3)
     u_spec, h_spec, d_spec = take(3)
-    f1_ref, f2_ref, g2_ref, g1_ref, tw_ref, win_ref = take(6)
-    z_own, d_own, x_peer, z_peer, d_peer, do_peer = take(6)
+    f1_ref, f2_ref, g2_ref, g1_ref, tw_ref, win_ref, wout_ref = take(7)
+    qkv_ref, dz_ref = take(2)
+    x_own, z_own, d_own, x_peer, z_peer, d_peer, do_peer = take(7)
     partial = take(6)
     vias, fins, reds = [], [], []
     for phase in range(3):
@@ -120,15 +122,22 @@
         filt_ref.at[pl.ds(i * per_slot, per_slot), pl.ds(first_lane, 128)], wide.at[i % n_slot], wide_sem.at[i])
         for i in range(n_wide)]
     loads = [pltpu.make_async_copy(src, dst, load_sem.at[i]) for i, (src, dst) in enumerate(
-        ((f1_hbm, f1_ref), (f2_hbm, f2_ref), (g2_hbm, g2_ref), (g1_hbm, g1_ref), (tw_hbm, tw_ref), (win_hbm, win_ref)))]
-    for copy in wides[:n_slot] + loads:
+        [(win_hbm.at[:, pl.ds(j * width, width)], win_ref.at[:, pl.ds(j * width, width)]) for j in range(3)]
+        + [(wout_hbm, wout_ref), (f1_hbm, f1_ref), (f2_hbm, f2_ref), (g2_hbm, g2_ref), (g1_hbm, g1_ref), (tw_hbm, tw_ref)])]
+    for copy in [loads[1], loads[2], loads[0]] + loads[3:] + wides[:n_slot]:
         copy.start()
 
     def act(i):
         return qkv_ref[i * width:(i + 1) * width]
 
+    def project(i):
+        loads[i].wait()
+        for first in range(i * width, (i + 1) * width, 256):
+            qkv_ref[first:first + 256] = dot(x_ref[...], win_ref[:, first:first + 256]).T.astype(BF16)
+
+    project(1)
+    project(2)
     u_out[...] = (act(1) * act(2)).reshape(u_out.shape)
-    dy_out[...] = (dz_ref[...] * act(0)).reshape(dy_out.shape)
     pl.semaphore_wait(barrier, n_dev - 1)
 
     def exchange(which, src, dst):
@@ -140,7 +149,17 @@
         pltpu.make_async_copy(part, part, sem.at[which]).wait()
 
     exchange(0, u_out, u_in)
+    project(0)
+    loads[3].wait()
+    for first in range(0, width, 256):
+        dz_ref[first:first + 256] = lax.dot_general(
+            do_ref[...], wout_ref[first:first + 256], (((1,), (1,)), ((), ())), preferred_element_type=F32).T.astype(BF16)
+    dy_out[...] = (dz_ref[...] * act(0)).reshape(dy_out.shape)
     exchange(1, dy_out, dy_in)
+    n_group = 256 // (2 * n_chans)
+    for i in range(width // 256):
+        x_own[i * n_group:(i + 1) * n_group] = x_ref[:, i * 256:(i + 1) * 256].astype(F32).T.astype(BF16).reshape(
+            n_group, 2, n_chans, n_tok)
 
     swaps = []
 
@@ -150,7 +169,7 @@
         swaps.append(copy)
         return copy
 
-    x_swap = swap(x_ref.at[:, 1 - core], x_peer)
+    x_swap = swap(x_own.at[:, 1 - core], x_peer)
     do_swap = swap(do_ref, do_peer)
 
     own_row = pl.multiple_of(lax.rem(rank * n_chans, 128), n_chans)
@@ -170,7 +189,7 @@
         lax.fori_loop(0, per_wide // 4, turn, 0)
         if i + n_slot < n_wide:
             wides[i + n_slot].start()
-    for copy in loads[:5]:
+    for copy in loads[4:]:
         copy.wait()
 
     def f1(i):
@@ -211,12 +230,12 @@
         th, tl = halves(jnp.concatenate([jnp.concatenate(tr, axis=1), jnp.concatenate(ti, axis=1)], axis=0))
         return dot(g1(0), th) + (dot(g1(0), tl) + dot(g1(1), th))
 
-    def pairs(body):
+    def pairs(body, first=0, last=n_pairs):
         def step(p, carry):
             body(p)
             return carry
 
-        lax.fori_loop(0, n_pairs, step, 0)
+        lax.fori_loop(first, last, step, 0)
 
     def rows_of(ref, chan):
         return jnp.concatenate([ref[0, pl.ds(chan, n_dev, stride=n_chans), :],
@@ -298,7 +317,7 @@
                 gfilt_ref[pl.ds(odd * n_chans + chan, n_dev, stride=2 * n_chans), :] = lin[
                     odd * n_dev:(odd + 1) * n_dev, cols]
 
-    pairs(taps_grad)
+    pairs(taps_grad, 0, n_pairs // 2)
 
     def at_offset(dim, step):
         pos = lax.rem(coords[dim] + step, RING)
@@ -335,7 +354,7 @@
                     val = (mm(flat(z_own[:, core]), do_ref[:, at:at + step], 0)
                            + mm(flat(z_peer[...]), do_peer[:, at:at + step], 0))
                 else:
-                    val = (mm(flat(x_ref[:, core]), d_own[at:at + step], 1)
+                    val = (mm(flat(x_own[:, core]), d_own[at:at + step], 1)
                            + mm(flat(x_peer[...]), d_peer[at:at + step], 1))
                 partial[part][:, :, :, :, place + off:place + off + step] = val.reshape(
                     RING, RING, RING, n_chans, step)
@@ -428,6 +447,7 @@
         products(part)
         launch(part, 0)
 
+    pairs(taps_grad, n_pairs // 2, n_pairs)
     wait_all(ex_recv, 3, du_in)
     du_act = du_in[...].reshape(width, n_tok)
     for i in (1, 2):
@@ -446,7 +466,6 @@
         products(part)
         launch(part, 0)
 
-    loads[5].wait()
     for first in range(0, width, 256):
         gx_ref[:, first:first + 256] = dot(win_ref[first:first + 256], d_own[...]).T.astype(gx_ref.dtype)
 
@@ -467,24 +486,27 @@
         copy.wait_send()
 
 
-def hyena_grads(qkv, dz, x_cm, d_out, filt_taps, skip_gain, w_in, n_dev):
-    n_chip, n_core, n_chans, n_tok = x_cm.shape
-    width = dz.shape[0]
+def hyena_grads(x_tok, d_out, filt_taps, skip_gain, w_in, w_out, n_dev):
+    n_tok, width = x_tok.shape
+    n_chans, n_chip = width // n_dev, n_dev // 2
     n_lanes, n_rows = n_tok // 2, 2 * n_dev
     n_taps = filt_taps.shape[0]
-    n_wide, n_slot = 8, 4
+    n_wide, n_slot = 16, 3
     tables = [jnp.asarray(tab) for tab in transform_tables(n_rows, n_lanes)]
     vmem = pl.BlockSpec(memory_space=pltpu.VMEM)
     hbm = pl.BlockSpec(memory_space=pl.ANY)
     widths = [hi - lo for lo, hi in part_columns(2 * width)] * 2
-    scratch = [pltpu.VMEM((n_dev, n_chans, n_tok), BF16)] * 8
+    pairs = pltpu.VMEM((n_chip, 2, n_chans, n_tok), BF16)
+    single = pltpu.VMEM((n_chip, n_chans, n_tok), BF16)
+    stack = pltpu.VMEM((3 * width, n_tok), BF16)
+    scratch = [pltpu.VMEM((n_dev, n_chans, n_tok), BF16)] * 6
     scratch += [pltpu.VMEM((2, width, n_lanes), F32)] * 3
     scratch += [pltpu.VMEM((n_slot, n_taps // n_wide, 128), F32), pltpu.VMEM((4, 128, n_lanes), F32),
                 pltpu.VMEM((n_rows * n_chans, n_lanes), F32)]
     scratch += [pltpu.VMEM((n_chans // 2, 2 * n_rows, 2 * n_lanes), F32)] * 3
-    scratch += [pltpu.VMEM(arr.shape, arr.dtype) for arr in tables + [w_in]]
-    scratch += [pltpu.VMEM(x_cm.shape, BF16), pltpu.VMEM(qkv.shape, BF16), pltpu.VMEM((n_chip, n_chans, n_tok), BF16),
-                pltpu.VMEM((n_chip, n_chans, n_tok), BF16), pltpu.VMEM(qkv.shape, BF16), pltpu.VMEM(d_out.shape, BF16)]
+    scratch += [pltpu.VMEM(arr.shape, arr.dtype) for arr in tables + [w_in, w_out]]
+    scratch += [stack, pltpu.VMEM((width, n_tok), BF16)]
+    scratch += [pairs, pairs, stack, single, single, stack, pltpu.VMEM(d_out.shape, BF16)]
     scratch += [pltpu.VMEM((RING,) * 3 + (n_chans, w), F32) for w in widths]
     for n_lead in (2, 1, 0):
         lead = (RING,) * n_lead
@@ -492,7 +514,7 @@
         scratch += [pltpu.VMEM((2,) + lead + (n_chans, w), F32) for w in widths]
         if n_lead:
             scratch += [pltpu.VMEM(lead + (n_chans, w), F32) for w in widths]
-    scratch += [pltpu.SemaphoreType.DMA((n,)) for n in (len(tables) + 1, n_wide, 4, 4, 6, 6, 108, 108)]
+    scratch += [pltpu.SemaphoreType.DMA((n,)) for n in (len(tables) + 4, n_wide, 4, 4, 6, 6, 108, 108)]
     return pl.pallas_call(
         hyena_kernel,
         out_shape=(
@@ -502,13 +524,13 @@
             jax.ShapeDtypeStruct((n_rows * n_chans, n_lanes), F32),
             jax.ShapeDtypeStruct((n_chans, n_lanes), F32),
         ),
-        in_specs=[vmem] * 4 + [hbm, pl.BlockSpec(memory_space=pltpu.SMEM)] + [hbm] * 6,
+        in_specs=[vmem] * 2 + [hbm, pl.BlockSpec(memory_space=pltpu.SMEM)] + [hbm] * 7,
         out_specs=(vmem,) * 5,
         scratch_shapes=scratch,
-        compiler_params=pltpu.CompilerParams(vmem_limit_bytes=63 * 2 ** 20, collective_id=0, has_side_effects=True),
+        compiler_params=pltpu.CompilerParams(vmem_limit_bytes=56 * 2 ** 20, collective_id=0, has_side_effects=True),
         cost_estimate=pl.CostEstimate(flops=2 * 10 ** 10, bytes_accessed=32 * 2 ** 20, transcendentals=0),
         name="hyena_grads",
-    )(qkv, dz, x_cm, d_out, filt_taps, skip_gain, w_in, *tables)
+    )(x_tok, d_out, filt_taps, skip_gain, w_in, w_out, *tables)
 
 
 def solution(mesh):
@@ -521,14 +543,8 @@
         n_lanes = n_tok // 2
         x_tok, do_tok = x_seq[0], d_out[0]
 
-        def mm(a, b, ca, cb):
-            return lax.dot_general(a, b, (((ca,), (cb,)), ((), ())), preferred_element_type=F32)
-
-        qkv = mm(w_in, x_tok, 0, 1).astype(BF16)
-        dz = mm(w_out, do_tok, 1, 1).astype(BF16)
-        x_cm = x_tok.T.reshape(ctx_size // 2, 2, n_chans, n_tok)
         grad_x, grad_w_in, grad_w_out, gfilt, gskip = hyena_grads(
-            qkv, dz, x_cm, do_tok, filt_taps, skip_gain, w_in, ctx_size)
+            x_tok, do_tok, filt_taps, skip_gain, w_in, w_out, ctx_size)
         grad_filt = gfilt.reshape(seq_len // n_lanes, n_chans, n_lanes).transpose(0, 2, 1).reshape(seq_len, n_chans)
         return grad_x[None], grad_w_in, grad_w_out, grad_filt, jnp.sum(gskip, axis=1)
 

time: 122 us -> 111 us (0.910)
  matrix products: 9.11 us -> 0 us
    dot_general x2 -> x0, matrix products: 9.11 us -> none  [mm(): lax.dot_general(a, b, (((ca,), (cb,)), ((), ())), preferred_element_type=...]
    unnamed x6 -> x4, local copies, waits for them, and re-layouts: 6.88 us -> 6.87 us
where the time goes in v4:
time: 111 us; the launch traced here: 110 us
  Pallas kernels  101 us (91%)
  local copies, waits for them, and re-layouts  6.87 us (6%)
  other arithmetic  1.3 us (1%)
    pallas_call x1, Pallas kernels, hyena_grads(): pl.pallas_call(hyena_kernel, out_shape=(jax.ShapeDtypeStruct((n_tok, widt...  101 us
    unnamed x4, local copies, waits for them, and re-layouts  6.87 us

profile of v4, /device:TPU:0, one launch (start us, length us, event | category | flops | bytes accessed | tf_op | source)
XLA Modules:
  0.0 110.3 jit_solution(2910794087056352992)
XLA Ops:
  0.6 101.5 %hyena_grads.1 = (bf16[256,1024]{1,0:T(8,128)(2,1)}, bf16[8,3072]{1,0:T(8,128)(2,1)}, bf16[8,1024]{1,0:T(8,128)(2,1)}, f32[2048,128]{1,0:T(8,128)}, f32[8,128]{1,0:T(8,128)}) custom-call(bf16[256,1024]{1,0:T(8,128)(2,1)} %bitcast.9, bf16[256,1024]{1,0:T(8,128)(2,1)} %bitcast.10, f32[32768,1024]{1,0:T(8,128)} %filt_ref.1, f32[1024]{0:T(1024)} %skip_ref.1, ...), custom_call_target="tpu_custom_call" | custom-call | flops 20000000000 | bytes 33554432 | tf_op jit(solution)/shard_map/hyena_grads/pallas_call | solution.py:518
  102.1 1.3 %reduce_sum.9 = f32[8]{0:T(128)} reduce(f32[8,128]{1,0:T(8,128)} %get-tuple-element.14, f32[]{:T(128)} %constant.5.clone.1), dimensions={1}, to_apply=%region_0.0 | reduce | flops 1016 | bytes 4132 | tf_op jit(solution)/shard_map/reduce_sum | solution.py:549
  103.4 1.9 %copy.20 = bf16[1,256,1024]{2,1,0:T(8,128)(2,1)} copy(bf16[1,256,1024]{2,1,0:T(8,128)(2,1)} %bitcast.11) | data formatting | bytes 1048576
  105.3 1.4 %copy.21 = bf16[8,3072]{1,0:T(8,128)(2,1)} copy(bf16[8,3072]{1,0:T(8,128)(2,1)} %get-tuple-element.21) | data formatting | bytes 98304
  106.7 1.3 %copy.22 = bf16[8,1024]{1,0:T(8,128)(2,1)} copy(bf16[8,1024]{1,0:T(8,128)(2,1)} %get-tuple-element.22) | data formatting | bytes 32768
  108.0 2.3 %copy.23 = f32[32768,8]{0,1:T(8,128)} copy(f32[32768,8]{0,1:T(8,128)} %bitcast.8) | data formatting | bytes 2097152

commit v5 on v4

--- a/solution.py
+++ b/solution.py
@@ -65,6 +65,32 @@
     return [(ends[i], ends[i + 1]) for i in range(3)]
 
 
+def all_columns(width):
+    cut = (2 * width // 128 * 5 + 7) // 8 * 128
+    return (part_columns(2 * width) + part_columns(cut)
+            + [(cut + lo, cut + hi) for lo, hi in part_columns(2 * width - cut)])
+
+
+def result_kernel(*refs):
+    for src, dst in zip(refs[:4], refs[5:9]):
+        dst[...] = src[...]
+    refs[9][...] = jnp.sum(refs[4][...].T, axis=0)
+
+
+def results(*vals):
+    vmem = pl.BlockSpec(memory_space=pltpu.VMEM)
+    n_chans = vals[4].shape[0]
+    return pl.pallas_call(
+        result_kernel,
+        out_shape=tuple(jax.ShapeDtypeStruct(val.shape, val.dtype) for val in vals[:4])
+        + (jax.ShapeDtypeStruct((n_chans,), F32),),
+        in_specs=[vmem] * 5,
+        out_specs=(vmem,) * 5,
+        cost_estimate=pl.CostEstimate(flops=10 ** 6, bytes_accessed=4 * 2 ** 20, transcendentals=0),
+        name="results",
+    )(*vals)
+
+
 def hyena_kernel(x_ref, do_ref, filt_ref, skip_ref, win_hbm, wout_hbm, f1_hbm, f2_hbm, g2_hbm, g1_hbm, tw_hbm,
                  gx_ref, gwin_ref, gwout_ref, gfilt_ref, gskip_ref, *scratch):
     names = iter(scratch)
@@ -80,13 +106,13 @@
     f1_ref, f2_ref, g2_ref, g1_ref, tw_ref, win_ref, wout_ref = take(7)
     qkv_ref, dz_ref = take(2)
     x_own, z_own, d_own, x_peer, z_peer, d_peer, do_peer = take(7)
-    partial = take(6)
+    partial = take(9)
     vias, fins, reds = [], [], []
     for phase in range(3):
-        vias.append(take(6))
-        fins.append(take(6))
+        vias.append(take(9))
+        fins.append(take(9))
         if phase < 2:
-            reds.append(take(6))
+            reds.append(take(9))
     load_sem, wide_sem, ex_send, ex_recv, swap_send, swap_recv, ring_send, ring_recv = take(8)
 
     n_dev, n_chans, n_tok = u_out.shape
@@ -106,11 +132,14 @@
                                             device_id={"cp": device}, device_id_type=pl.DeviceIdType.MESH)
 
     def others(body):
+        body(lax.rem(rank + 1, n_dev))
+
         def step(i, carry):
-            body(lax.rem(rank + i, n_dev))
+            for k in range(7):
+                body(lax.rem(rank + 2 + 7 * i + k, n_dev))
             return carry
 
-        lax.fori_loop(1, n_dev, step, 0)
+        lax.fori_loop(0, (n_dev - 2) // 7, step, 0)
 
     barrier = pltpu.get_barrier_semaphore()
     others(lambda dev: pl.semaphore_signal(barrier, inc=1, device_id={"cp": dev}, device_id_type=pl.DeviceIdType.MESH))
@@ -326,7 +355,7 @@
     nxt = [at_offset(dim, 1) for dim in range(3)]
     opp = [at_offset(dim, 2) for dim in range(3)]
     prv = [at_offset(dim, 3) for dim in range(3)]
-    cols = part_columns(2 * width)
+    cols = all_columns(width)
     half_rows = width // 2
 
     def mm(a, b, cb):
@@ -336,7 +365,7 @@
         return val.reshape(half_rows, n_tok)
 
     def segments(part):
-        lo, hi = cols[part % 3]
+        lo, hi = cols[part]
         runs = []
         for first, is_out, base in (((0, False, 0), (width, True, 0)) if part < 3 else ((0, False, width),)):
             last = first + width if part < 3 else 2 * width
@@ -370,7 +399,7 @@
     copies = {}
 
     def send(part, phase, which, src, dst, device):
-        slot = (phase * 6 + part) * 6 + which
+        slot = (phase * 9 + part) * 6 + which
         copy = remote(src, dst, ring_send.at[slot], ring_recv.at[slot], device)
         copy.start()
         copies[part, phase, which] = copy
@@ -440,7 +469,7 @@
         if phase < 2:
             launch(part, phase + 1)
 
-    early, late = (0, 1, 2), (3, 4, 5)
+    early, late, last = (0, 1, 2), (3, 4, 5), (6, 7, 8)
     for copy in (x_swap, do_swap, z_swap, d_swaps[0]):
         copy.wait_recv()
     for part in early:
@@ -465,21 +494,30 @@
     for part in late:
         products(part)
         launch(part, 0)
+    for part in last:
+        products(part)
 
     for first in range(0, width, 256):
         gx_ref[:, first:first + 256] = dot(win_ref[first:first + 256], d_own[...]).T.astype(gx_ref.dtype)
 
     run(finish, early, 0)
     run(relay, late, 0)
+    run(launch, last, 0)
     run(relay, early, 1)
     run(finish, early, 1)
     run(finish, late, 0)
+    run(relay, last, 0)
     run(relay, early, 2)
     run(finish, early, 2)
     run(relay, late, 1)
     run(finish, late, 1)
+    run(finish, last, 0)
     run(relay, late, 2)
     run(finish, late, 2)
+    run(relay, last, 1)
+    run(finish, last, 1)
+    run(relay, last, 2)
+    run(finish, last, 2)
     for which, ref in enumerate((u_out, dy_out, y_out, du_out)):
         wait_all(ex_send, which, ref)
     for copy in list(copies.values()) + swaps:
@@ -495,7 +533,7 @@
     tables = [jnp.asarray(tab) for tab in transform_tables(n_rows, n_lanes)]
     vmem = pl.BlockSpec(memory_space=pltpu.VMEM)
     hbm = pl.BlockSpec(memory_space=pl.ANY)
-    widths = [hi - lo for lo, hi in part_columns(2 * width)] * 2
+    widths = [hi - lo for lo, hi in all_columns(width)]
     pairs = pltpu.VMEM((n_chip, 2, n_chans, n_tok), BF16)
     single = pltpu.VMEM((n_chip, n_chans, n_tok), BF16)
     stack = pltpu.VMEM((3 * width, n_tok), BF16)
@@ -514,7 +552,7 @@
         scratch += [pltpu.VMEM((2,) + lead + (n_chans, w), F32) for w in widths]
         if n_lead:
             scratch += [pltpu.VMEM(lead + (n_chans, w), F32) for w in widths]
-    scratch += [pltpu.SemaphoreType.DMA((n,)) for n in (len(tables) + 4, n_wide, 4, 4, 6, 6, 108, 108)]
+    scratch += [pltpu.SemaphoreType.DMA((n,)) for n in (len(tables) + 4, n_wide, 4, 4, 6, 6, 162, 162)]
     return pl.pallas_call(
         hyena_kernel,
         out_shape=(
@@ -527,7 +565,7 @@
         in_specs=[vmem] * 2 + [hbm, pl.BlockSpec(memory_space=pltpu.SMEM)] + [hbm] * 7,
         out_specs=(vmem,) * 5,
         scratch_shapes=scratch,
-        compiler_params=pltpu.CompilerParams(vmem_limit_bytes=56 * 2 ** 20, collective_id=0, has_side_effects=True),
+        compiler_params=pltpu.CompilerParams(vmem_limit_bytes=57 * 2 ** 20, collective_id=0, has_side_effects=True),
         cost_estimate=pl.CostEstimate(flops=2 * 10 ** 10, bytes_accessed=32 * 2 ** 20, transcendentals=0),
         name="hyena_grads",
     )(x_tok, d_out, filt_taps, skip_gain, w_in, w_out, *tables)
@@ -543,10 +581,10 @@
         n_lanes = n_tok // 2
         x_tok, do_tok = x_seq[0], d_out[0]
 
-        grad_x, grad_w_in, grad_w_out, gfilt, gskip = hyena_grads(
-            x_tok, do_tok, filt_taps, skip_gain, w_in, w_out, ctx_size)
+        grad_x, grad_w_in, grad_w_out, gfilt, grad_skip = results(*hyena_grads(
+            x_tok, do_tok, filt_taps, skip_gain, w_in, w_out, ctx_size))
         grad_filt = gfilt.reshape(seq_len // n_lanes, n_chans, n_lanes).transpose(0, 2, 1).reshape(seq_len, n_chans)
-        return grad_x[None], grad_w_in, grad_w_out, grad_filt, jnp.sum(gskip, axis=1)
+        return grad_x[None], grad_w_in, grad_w_out, grad_filt, grad_skip
 
     seq_spec = P("dp", "cp", None)
     row_spec = P(("dp", "cp"), None)

time: 111 us -> 113 us (1.018)
  Pallas kernels: 101 us -> 112 us
  local copies, waits for them, and re-layouts: 6.87 us -> 0 us
  other arithmetic: 1.3 us -> 0 us
    pallas_call x1, Pallas kernels: 101 us -> 109 us  [hyena_grads(): pl.pallas_call(hyena_kernel, out_shape=(jax.ShapeDtypeStruct((n_tok, widt...]
    unnamed x4 -> x0, local copies, waits for them, and re-layouts: 6.87 us -> none
    pallas_call x0 -> x1, Pallas kernels: none -> 2.61 us  [results(): pl.pallas_call(result_kernel, out_shape=tuple((jax.ShapeDtypeStruct(val.s...]
    reduce_sum x1 -> x0, other arithmetic: 1.3 us -> none  [local_step(): jnp.sum(gskip, axis=1)]
where the time goes in v5:
time: 113 us
  Pallas kernels  112 us (99%)
    pallas_call x1, Pallas kernels, hyena_grads(): pl.pallas_call(hyena_kernel, out_shape=(jax.ShapeDtypeStruct((n_tok, widt...  109 us
    pallas_call x1, Pallas kernels, results(): pl.pallas_call(result_kernel, out_shape=tuple((jax.ShapeDtypeStruct(val.s...  2.61 us

profile of v5, /device:TPU:0, one launch (start us, length us, event | category | flops | bytes accessed | tf_op | source)
XLA Modules:
  0.0 112.5 jit_solution(12973307815616834381)
XLA Ops:
  0.6 109.3 %hyena_grads.1 = (bf16[256,1024]{1,0:T(8,128)(2,1)}, bf16[8,3072]{1,0:T(8,128)(2,1)}, bf16[8,1024]{1,0:T(8,128)(2,1)}, f32[2048,128]{1,0:T(8,128)}, f32[8,128]{1,0:T(8,128)}) custom-call(bf16[256,1024]{1,0:T(8,128)(2,1)} %bitcast.8, bf16[256,1024]{1,0:T(8,128)(2,1)} %bitcast.9, f32[32768,1024]{1,0:T(8,128)} %filt_ref.1, f32[1024]{0:T(1024)} %skip_ref.1, ...), custom_call_target="tpu_custom_call" | custom-call | flops 20000000000 | bytes 33554432 | tf_op jit(solution)/shard_map/hyena_grads/pallas_call | solution.py:556
  109.9 2.6 %results.1 = (bf16[256,1024]{1,0:T(8,128)(2,1)}, bf16[8,3072]{1,0:T(8,128)(2,1)}, bf16[8,1024]{1,0:T(8,128)(2,1)}, f32[2048,128]{1,0:T(8,128)}, f32[8]{0:T(128)}) custom-call(bf16[256,1024]{1,0:T(8,128)(2,1)} %get-tuple-element.15.refs_0_, bf16[8,3072]{1,0:T(8,128)(2,1)} %get-tuple-element.16.refs_1_, bf16[8,1024]{1,0:T(8,128)(2,1)} %get-tuple-element.17.refs_2_, ...), custom_call_target="tpu_custom_call" | custom-call | flops 1000000 | bytes 4194304 | tf_op jit(solution)/shard_map/results/pallas_call | solution.py:83

commit v6 on v5

--- a/solution.py
+++ b/solution.py
@@ -66,9 +66,7 @@
 
 
 def all_columns(width):
-    cut = (2 * width // 128 * 5 + 7) // 8 * 128
-    return (part_columns(2 * width) + part_columns(cut)
-            + [(cut + lo, cut + hi) for lo, hi in part_columns(2 * width - cut)])
+    return part_columns(2 * width) * 2
 
 
 def result_kernel(*refs):
@@ -106,13 +104,13 @@
     f1_ref, f2_ref, g2_ref, g1_ref, tw_ref, win_ref, wout_ref = take(7)
     qkv_ref, dz_ref = take(2)
     x_own, z_own, d_own, x_peer, z_peer, d_peer, do_peer = take(7)
-    partial = take(9)
+    partial = take(6)
     vias, fins, reds = [], [], []
     for phase in range(3):
-        vias.append(take(9))
-        fins.append(take(9))
+        vias.append(take(6))
+        fins.append(take(6))
         if phase < 2:
-            reds.append(take(9))
+            reds.append(take(6))
     load_sem, wide_sem, ex_send, ex_recv, swap_send, swap_recv, ring_send, ring_recv = take(8)
 
     n_dev, n_chans, n_tok = u_out.shape
@@ -399,7 +397,7 @@
     copies = {}
 
     def send(part, phase, which, src, dst, device):
-        slot = (phase * 9 + part) * 6 + which
+        slot = (phase * 6 + part) * 6 + which
         copy = remote(src, dst, ring_send.at[slot], ring_recv.at[slot], device)
         copy.start()
         copies[part, phase, which] = copy
@@ -469,14 +467,13 @@
         if phase < 2:
             launch(part, phase + 1)
 
-    early, late, last = (0, 1, 2), (3, 4, 5), (6, 7, 8)
+    early, late = (0, 1, 2), (3, 4, 5)
     for copy in (x_swap, do_swap, z_swap, d_swaps[0]):
         copy.wait_recv()
     for part in early:
         products(part)
         launch(part, 0)
 
-    pairs(taps_grad, n_pairs // 2, n_pairs)
     wait_all(ex_recv, 3, du_in)
     du_act = du_in[...].reshape(width, n_tok)
     for i in (1, 2):
@@ -494,30 +491,26 @@
     for part in late:
         products(part)
         launch(part, 0)
-    for part in last:
-        products(part)
-
-    for first in range(0, width, 256):
+    pairs(taps_grad, n_pairs // 2, n_pairs)
+
+    def input_grad(first):
         gx_ref[:, first:first + 256] = dot(win_ref[first:first + 256], d_own[...]).T.astype(gx_ref.dtype)
 
     run(finish, early, 0)
     run(relay, late, 0)
-    run(launch, last, 0)
     run(relay, early, 1)
     run(finish, early, 1)
     run(finish, late, 0)
-    run(relay, last, 0)
+    input_grad(0)
+    input_grad(256)
     run(relay, early, 2)
     run(finish, early, 2)
     run(relay, late, 1)
+    input_grad(512)
     run(finish, late, 1)
-    run(finish, last, 0)
+    input_grad(768)
     run(relay, late, 2)
     run(finish, late, 2)
-    run(relay, last, 1)
-    run(finish, last, 1)
-    run(relay, last, 2)
-    run(finish, last, 2)
     for which, ref in enumerate((u_out, dy_out, y_out, du_out)):
         wait_all(ex_send, which, ref)
     for copy in list(copies.values()) + swaps:
@@ -552,7 +545,7 @@
         scratch += [pltpu.VMEM((2,) + lead + (n_chans, w), F32) for w in widths]
         if n_lead:
             scratch += [pltpu.VMEM(lead + (n_chans, w), F32) for w in widths]
-    scratch += [pltpu.SemaphoreType.DMA((n,)) for n in (len(tables) + 4, n_wide, 4, 4, 6, 6, 162, 162)]
+    scratch += [pltpu.SemaphoreType.DMA((n,)) for n in (len(tables) + 4, n_wide, 4, 4, 6, 6, 108, 108)]
     return pl.pallas_call(
         hyena_kernel,
         out_shape=(

time: 113 us -> 104 us (0.920)
  Pallas kernels: 112 us -> 103 us
    pallas_call x1, Pallas kernels: 109 us -> 100 us  [hyena_grads(): pl.pallas_call(hyena_kernel, out_shape=(jax.ShapeDtypeStruct((n_tok, widt...]
where the time goes in v6:
time: 104 us; the launch traced here: 103 us
  Pallas kernels  103 us (99%)
    pallas_call x1, Pallas kernels, hyena_grads(): pl.pallas_call(hyena_kernel, out_shape=(jax.ShapeDtypeStruct((n_tok, widt...  100 us
    pallas_call x1, Pallas kernels, results(): pl.pallas_call(result_kernel, out_shape=tuple((jax.ShapeDtypeStruct(val.s...  2.61 us

profile of v6, /device:TPU:0, one launch (start us, length us, event | category | flops | bytes accessed | tf_op | source)
XLA Modules:
  0.0 103.2 jit_solution(13639794152226794153)
XLA Ops:
  0.6 100.0 %hyena_grads.1 = (bf16[256,1024]{1,0:T(8,128)(2,1)}, bf16[8,3072]{1,0:T(8,128)(2,1)}, bf16[8,1024]{1,0:T(8,128)(2,1)}, f32[2048,128]{1,0:T(8,128)}, f32[8,128]{1,0:T(8,128)}) custom-call(bf16[256,1024]{1,0:T(8,128)(2,1)} %bitcast.8, bf16[256,1024]{1,0:T(8,128)(2,1)} %bitcast.9, f32[32768,1024]{1,0:T(8,128)} %filt_ref.1, f32[1024]{0:T(1024)} %skip_ref.1, ...), custom_call_target="tpu_custom_call" | custom-call | flops 20000000000 | bytes 33554432 | tf_op jit(solution)/shard_map/hyena_grads/pallas_call | solution.py:549
  100.6 2.6 %results.1 = (bf16[256,1024]{1,0:T(8,128)(2,1)}, bf16[8,3072]{1,0:T(8,128)(2,1)}, bf16[8,1024]{1,0:T(8,128)(2,1)}, f32[2048,128]{1,0:T(8,128)}, f32[8]{0:T(128)}) custom-call(bf16[256,1024]{1,0:T(8,128)(2,1)} %get-tuple-element.15.refs_0_, bf16[8,3072]{1,0:T(8,128)(2,1)} %get-tuple-element.16.refs_1_, bf16[8,1024]{1,0:T(8,128)(2,1)} %get-tuple-element.17.refs_2_, ...), custom_call_target="tpu_custom_call" | custom-call | flops 1000000 | bytes 4194304 | tf_op jit(solution)/shard_map/results/pallas_call | solution.py:81

commit v7 on v6

--- a/solution.py
+++ b/solution.py
@@ -522,7 +522,7 @@
     n_chans, n_chip = width // n_dev, n_dev // 2
     n_lanes, n_rows = n_tok // 2, 2 * n_dev
     n_taps = filt_taps.shape[0]
-    n_wide, n_slot = 16, 3
+    n_wide, n_slot = 16, 8
     tables = [jnp.asarray(tab) for tab in transform_tables(n_rows, n_lanes)]
     vmem = pl.BlockSpec(memory_space=pltpu.VMEM)
     hbm = pl.BlockSpec(memory_space=pl.ANY)
@@ -558,7 +558,7 @@
         in_specs=[vmem] * 2 + [hbm, pl.BlockSpec(memory_space=pltpu.SMEM)] + [hbm] * 7,
         out_specs=(vmem,) * 5,
         scratch_shapes=scratch,
-        compiler_params=pltpu.CompilerParams(vmem_limit_bytes=57 * 2 ** 20, collective_id=0, has_side_effects=True),
+        compiler_params=pltpu.CompilerParams(vmem_limit_bytes=62 * 2 ** 20, collective_id=0, has_side_effects=True),
         cost_estimate=pl.CostEstimate(flops=2 * 10 ** 10, bytes_accessed=32 * 2 ** 20, transcendentals=0),
         name="hyena_grads",
     )(x_tok, d_out, filt_taps, skip_gain, w_in, w_out, *tables)

time: 104 us -> 103 us (level)
  no operation moved by 1% of the time
where the time goes in v7:
time: 103 us
  Pallas kernels  103 us (100%)
    pallas_call x1, Pallas kernels, hyena_grads(): pl.pallas_call(hyena_kernel, out_shape=(jax.ShapeDtypeStruct((n_tok, widt...  100 us
    pallas_call x1, Pallas kernels, results(): pl.pallas_call(result_kernel, out_shape=tuple((jax.ShapeDtypeStruct(val.s...  2.61 us

profile of v7, /device:TPU:0, one launch (start us, length us, event | category | flops | bytes accessed | tf_op | source)
XLA Modules:
  0.0 103.2 jit_solution(7154934560478713330)
XLA Ops:
  0.6 100.0 %hyena_grads.1 = (bf16[256,1024]{1,0:T(8,128)(2,1)}, bf16[8,3072]{1,0:T(8,128)(2,1)}, bf16[8,1024]{1,0:T(8,128)(2,1)}, f32[2048,128]{1,0:T(8,128)}, f32[8,128]{1,0:T(8,128)}) custom-call(bf16[256,1024]{1,0:T(8,128)(2,1)} %bitcast.8, bf16[256,1024]{1,0:T(8,128)(2,1)} %bitcast.9, f32[32768,1024]{1,0:T(8,128)} %filt_ref.1, f32[1024]{0:T(1024)} %skip_ref.1, ...), custom_call_target="tpu_custom_call" | custom-call | flops 20000000000 | bytes 33554432 | tf_op jit(solution)/shard_map/hyena_grads/pallas_call | solution.py:549
  100.6 2.6 %results.1 = (bf16[256,1024]{1,0:T(8,128)(2,1)}, bf16[8,3072]{1,0:T(8,128)(2,1)}, bf16[8,1024]{1,0:T(8,128)(2,1)}, f32[2048,128]{1,0:T(8,128)}, f32[8]{0:T(128)}) custom-call(bf16[256,1024]{1,0:T(8,128)(2,1)} %get-tuple-element.15.refs_0_, bf16[8,3072]{1,0:T(8,128)(2,1)} %get-tuple-element.16.refs_1_, bf16[8,1024]{1,0:T(8,128)(2,1)} %get-tuple-element.17.refs_2_, ...), custom_call_target="tpu_custom_call" | custom-call | flops 1000000 | bytes 4194304 | tf_op jit(solution)/shard_map/results/pallas_call | solution.py:81

commit v8 on v7

--- a/solution.py
+++ b/solution.py
@@ -501,11 +501,11 @@
     run(relay, early, 1)
     run(finish, early, 1)
     run(finish, late, 0)
+    run(relay, early, 2)
     input_grad(0)
     input_grad(256)
-    run(relay, early, 2)
+    run(relay, late, 1)
     run(finish, early, 2)
-    run(relay, late, 1)
     input_grad(512)
     run(finish, late, 1)
     input_grad(768)

time: 103 us -> 101 us (0.981)
  Pallas kernels: 103 us -> 100 us
    pallas_call x1, Pallas kernels: 100 us -> 97.6 us  [hyena_grads(): pl.pallas_call(hyena_kernel, out_shape=(jax.ShapeDtypeStruct((n_tok, widt...]
where the time goes in v8:
time: 101 us
  Pallas kernels  100 us (99%)
    pallas_call x1, Pallas kernels, hyena_grads(): pl.pallas_call(hyena_kernel, out_shape=(jax.ShapeDtypeStruct((n_tok, widt...  97.6 us
    pallas_call x1, Pallas kernels, results(): pl.pallas_call(result_kernel, out_shape=tuple((jax.ShapeDtypeStruct(val.s...  2.61 us

profile of v8, /device:TPU:0, one launch (start us, length us, event | category | flops | bytes accessed | tf_op | source)
XLA Modules:
  0.0 100.9 jit_solution(13550547764935192014)
XLA Ops:
  0.6 97.6 %hyena_grads.1 = (bf16[256,1024]{1,0:T(8,128)(2,1)}, bf16[8,3072]{1,0:T(8,128)(2,1)}, bf16[8,1024]{1,0:T(8,128)(2,1)}, f32[2048,128]{1,0:T(8,128)}, f32[8,128]{1,0:T(8,128)}) custom-call(bf16[256,1024]{1,0:T(8,128)(2,1)} %bitcast.8, bf16[256,1024]{1,0:T(8,128)(2,1)} %bitcast.9, f32[32768,1024]{1,0:T(8,128)} %filt_ref.1, f32[1024]{0:T(1024)} %skip_ref.1, ...), custom_call_target="tpu_custom_call" | custom-call | flops 20000000000 | bytes 33554432 | tf_op jit(solution)/shard_map/hyena_grads/pallas_call | solution.py:549
  98.3 2.6 %results.1 = (bf16[256,1024]{1,0:T(8,128)(2,1)}, bf16[8,3072]{1,0:T(8,128)(2,1)}, bf16[8,1024]{1,0:T(8,128)(2,1)}, f32[2048,128]{1,0:T(8,128)}, f32[8]{0:T(128)}) custom-call(bf16[256,1024]{1,0:T(8,128)(2,1)} %get-tuple-element.15.refs_0_, bf16[8,3072]{1,0:T(8,128)(2,1)} %get-tuple-element.16.refs_1_, bf16[8,1024]{1,0:T(8,128)(2,1)} %get-tuple-element.17.refs_2_, ...), custom_call_target="tpu_custom_call" | custom-call | flops 1000000 | bytes 4194304 | tf_op jit(solution)/shard_map/results/pallas_call | solution.py:81
